TPU v7x, 32 devices: a whole 2x2x4 slice. The times are simulated.
32 devices in a mesh: dp: 4 (over z), tp: 8 (over y, x, core).
Axes of the slice: x: 2, y: 2, z: 4, core: 2. Of those that a mesh axis runs over, the one named last changes fastest.
Arguments:
- hidden: bfloat16 [512, 128, 1024], P('dp')
- positions: int32 [512, 20], P('dp')
- labels: int32 [512, 20], P('dp')
- weights: float32 [512, 20], P('dp')
- w_t: bfloat16 [1024, 1024], replicated
- b_t: float32 [1024], replicated
- gamma: float32 [1024], replicated
- beta: float32 [1024], replicated
- embed: bfloat16 [30592, 1024], P('tp')
- out_bias: float32 [30592], P('tp')
Outputs:
- output 1: float32 [], replicated
- output 2: bfloat16 [512, 128, 1024], P('dp')
- output 3: float32 [1024, 1024], replicated
- output 4: float32 [1024], replicated
- output 5: float32 [1024], replicated
- output 6: float32 [1024], replicated
- output 7: float32 [30592, 1024], P('tp')
- output 8: float32 [30592], P('tp')
All inputs are finite; a program needn't handle non-finite values.
Results may differ from a plain program's by a relative error of at most 0.001.
Values sent between devices are 32-bit elements.
A program may use at most 1 GiB of HBM per device.

v0:
```python
import jax
import jax.numpy as jnp
from jax import lax
from jax.sharding import PartitionSpec as P

LN_EPS = 1e-12
LOSS_EPS = 1e-5


def gelu_norm(pre_act, gamma, beta):
    activated = jax.nn.gelu(pre_act, approximate=False)
    mean_val = jnp.mean(activated, axis=-1, keepdims=True)
    centered = activated - mean_val
    variance = jnp.mean(centered * centered, axis=-1, keepdims=True)
    return centered * lax.rsqrt(variance + LN_EPS) * gamma + beta


def solution(mesh):
    def local_step(hidden, positions, labels, weights, w_t, b_t, gamma, beta, embed, out_bias):
        batch, seq_len, width = hidden.shape
        max_pred = positions.shape[1]
        shard_vocab = embed.shape[0]
        pos_hot = (positions[:, :, None] == jnp.arange(seq_len, dtype=jnp.int32)[None, None, :]).astype(jnp.bfloat16)
        picked = jnp.einsum("bps,bsd->bpd", pos_hot, hidden, preferred_element_type=jnp.float32).astype(jnp.bfloat16)
        tok_rows = picked.reshape(batch * max_pred, width)
        pre_act = jnp.dot(tok_rows, w_t, preferred_element_type=jnp.float32) + b_t
        normed, norm_vjp = jax.vjp(gelu_norm, pre_act, gamma, beta)
        t_bf = normed.astype(jnp.bfloat16)
        logits = jnp.einsum("nd,vd->nv", t_bf, embed, preferred_element_type=jnp.float32) + out_bias
        row_max = lax.pmax(jnp.max(logits, axis=1), "tp")
        shifted = jnp.exp(logits - row_max[:, None])
        sum_exp = lax.psum(jnp.sum(shifted, axis=1), "tp")
        local_lab = labels.reshape(-1) - lax.axis_index("tp") * shard_vocab
        lab_hot = local_lab[:, None] == jnp.arange(shard_vocab, dtype=jnp.int32)[None, :]
        target_logit = lax.psum(jnp.sum(jnp.where(lab_hot, logits, 0.0), axis=1), "tp")
        flat_w = weights.reshape(-1)
        denom = lax.psum(jnp.sum(flat_w), "dp") + LOSS_EPS
        log_norm = jnp.log(sum_exp) + row_max
        loss = lax.psum(jnp.sum(flat_w * (log_norm - target_logit)), "dp") / denom
        soft_probs = shifted * (1.0 / sum_exp)[:, None]
        d_logits = jnp.where(lab_hot, soft_probs - 1.0, soft_probs) * (flat_w / denom)[:, None]
        dz_bf = d_logits.astype(jnp.bfloat16)
        d_embed = lax.psum(jnp.einsum("nv,nd->vd", dz_bf, t_bf, preferred_element_type=jnp.float32), "dp")
        d_out_bias = lax.psum(jnp.sum(d_logits, axis=0), "dp")
        d_normed = lax.psum(jnp.einsum("nv,vd->nd", dz_bf, embed, preferred_element_type=jnp.float32), "tp")
        d_pre, d_gamma, d_beta = norm_vjp(d_normed)
        d_pre_bf = d_pre.astype(jnp.bfloat16)
        d_w_t = lax.psum(jnp.einsum("nd,ne->de", tok_rows, d_pre_bf, preferred_element_type=jnp.float32), "dp")
        d_b_t = lax.psum(jnp.sum(d_pre, axis=0), "dp")
        d_gamma = lax.psum(d_gamma, "dp")
        d_beta = lax.psum(d_beta, "dp")
        d_rows = jnp.einsum("ne,de->nd", d_pre_bf, w_t, preferred_element_type=jnp.float32).astype(jnp.bfloat16)
        d_hidden = jnp.einsum("bps,bpd->bsd", pos_hot, d_rows.reshape(batch, max_pred, width), preferred_element_type=jnp.float32).astype(jnp.bfloat16)
        return loss, d_hidden, d_w_t, d_b_t, d_gamma, d_beta, d_embed, d_out_bias

    in_specs = (P("dp", None, None), P("dp", None), P("dp", None), P("dp", None), P(None, None), P(None), P(None), P(None), P("tp", None), P("tp"))
    out_specs = (P(), P("dp", None, None), P(None, None), P(None), P(None), P(None), P("tp", None), P("tp"))
    return jax.shard_map(local_step, mesh=mesh, in_specs=in_specs, out_specs=out_specs, check_vma=False)
```

profile of v0, /device:TPU:0, one launch (start us, length us, event | category | flops | bytes accessed | tf_op | source)
XLA Modules:
  0.0 1117.4 jit_solution(4545001985138017469)
XLA Ops:
  7.2 0.0 copy-start
  7.2 0.0 all-reduce.5.cloned.1.call-start
  7.2 0.9 copy.20
  8.2 1.3 reduce_sum.129
  9.5 14.1 %psum.80 = f32[]{:T(128)} all-reduce(f32[]{:T(128)} %reduce_sum.129), channel_id=1, replica_groups=mesh['dp'=4,'tp'=8] {'dp'}, use_global_device_ids=true, to_apply=%region_11.12 | all-reduce | flops 1 | bytes 8 | tf_op jit(solution)/shard_map/psum | solution.py:37
  23.6 0.7 broadcast_subtract_fusion
  24.3 0.1 copy.22
  24.4 0.1 sub.42
  24.5 0.8 copy.21
  25.4 0.0 copy-start.4
  25.4 0.1 reshape.75
  25.5 15.7 %convolution_convert_fusion.2 = bf16[128,20,1024]{2,1,0:T(8,128)(2,1)} fusion(bf16[128,128,1024]{2,1,0:T(8,128)(2,1)} %param.10, s32[128,20]{1,0:T(8,128)S(1)} %copy.21), kind=kOutput, calls=%fused_computation.34 | convolution fusion | flops 674037760 | bytes 38807552 | tf_op jit(solution)/shard_map/bps,bsd->bpd/dot_general | solution.py:24
  41.2 0.0 copy-done.4
  41.2 0.0 copy-start.10
  41.2 9.0 reshape.76
  50.2 0.0 copy-done
  50.2 0.0 copy-done.10
  50.2 32.5 %fusion.21 = (f32[2560]{0:T(1024)S(1)}, f32[2560,1024]{0,1:T(8,128)S(1)}, f32[2560,1024]{0,1:T(8,128)}, f32[2560,1024]{0,1:T(8,128)}) fusion(f32[1024]{0:T(1024)S(1)} %copy-done.10, bf16[2560,1024]{1,0:T(8,128)(2,1)} %reshape.76, bf16[1024,1024]{1,0:T(8,128)(2,1)S(1)} %copy-done), kind=kOutput, calls=%fused_computation.54 | convolution fusion | flops 5541721600 | bytes 38811648 | tf_op jit(solution)/shard_map/dot_general | solution.py:26
  82.7 0.0 copy-start.1
  82.7 0.0 copy-start.8
  82.7 0.0 copy-start.12
  82.7 1.1 multiply_reduce_fusion.2
  83.8 0.0 copy-start.6
  83.9 0.0 copy-done.8
  83.9 0.0 copy-done.9
  83.9 0.0 copy-done.12
  83.9 36.9 %add_reduce_fusion = (f32[2560]{0:T(1024)S(1)}, f32[2560,3824]{0,1:T(8,128)}) fusion(f32[3824]{0:T(1024)S(1)} %copy-done.8, bf16[3824,1024]{1,0:T(8,128)(2,1)} %param.18, f32[2560,1024]{0,1:T(8,128)S(1)} %get-tuple-element.24, f32[1024]{0:T(1024)S(1)} %copy-done.12, f32[1024]{0:T(1024)S(1)} %copy-done.9, f32[2560]{0:T(1024)S(1)} %fusion.16, ...), kind=kOutput, calls=%fused_computation.6 | convolution fusion | flops 20081457152 | bytes 57529280 | tf_op jit(solution)/shard_map/nd,vd->nv/dot_general | solution.py:29
  120.7 0.0 copy-done.1
  120.7 0.0 copy-done.6
  120.8 22.3 %pmax.7 = f32[2560]{0:T(1024)S(1)} all-reduce(f32[2560]{0:T(1024)S(1)} %get-tuple-element.28), channel_id=1, replica_groups=mesh['dp'=4,'tp'=8] {'tp'}, use_global_device_ids=true, to_apply=%region_3.0 | all-reduce | flops 2560 | bytes 20480 | tf_op jit(solution)/shard_map/pmax | solution.py:30
  143.1 16.7 %fusion.1 = f32[2560]{0:T(1024)S(1)} fusion(f32[2560,3824]{0,1:T(8,128)} %get-tuple-element.29, f32[2560]{0:T(1024)S(1)} %pmax.7, f32[3824]{0:T(1024)S(1)} %copy-done.8), kind=kLoop, calls=%fused_computation.5 | loop fusion | flops 29365760 | bytes 39193536 | tf_op jit(solution)/shard_map/reduce_sum | solution.py:32
  159.8 22.4 %psum.77 = f32[2560]{0:T(1024)S(1)} all-reduce(f32[2560]{0:T(1024)S(1)} %fusion.1), channel_id=1, replica_groups=mesh['dp'=4,'tp'=8] {'tp'}, use_global_device_ids=true, to_apply=%region_5.0 | all-reduce | flops 2560 | bytes 20480 | tf_op jit(solution)/shard_map/psum | solution.py:32
  182.8 30.2 %fusion.2 = (f32[3824]{0:T(1024)S(1)}, f32[2560]{0:T(1024)S(1)}, bf16[2560,3824]{0,1:T(8,128)(2,1)}) fusion(f32[2560,3824]{0,1:T(8,128)} %get-tuple-element.29, f32[2560]{0:T(1024)S(1)} %broadcast_divide_fusion, f32[2560]{0:T(1024)S(1)} %broadcast_divide_fusion.1, s32[2560]{0:T(1024)S(1)} %sub.42, f32[2560]{0:T(1024)S(1)} %pmax.7, f32[3824]{0:T(1024)S(1)} %copy-done.8), kind=kLoop, calls=%fused_computation.8 | loop fusion | flops 107677456 | bytes 58818432 | tf_op jit(solution)/shard_map/reduce_sum | solution.py:44
  212.9 27.2 %fusion.23 = f32[2560,1024]{0,1:T(8,128)} fusion(bf16[2560,3824]{0,1:T(8,128)(2,1)} %get-tuple-element.26, bf16[3824,1024]{1,0:T(8,128)(2,1)} %param.18), kind=kOutput, calls=%fused_computation.55 | convolution fusion | flops 20048773120 | bytes 37896192 | tf_op jit(solution)/shard_map/nv,vd->nd/dot_general | solution.py:45
  240.2 0.0 all-reduce.5.cloned.1.call-update
  240.2 0.0 all-reduce.7.cloned.1.call-start
  240.2 29.4 %fusion.17 = f32[3824,1024]{1,0:T(8,128)} fusion(bf16[2560,3824]{0,1:T(8,128)(2,1)} %get-tuple-element.26, f32[2560,1024]{0,1:T(8,128)} %copy-done.1, f32[1024]{0:T(1024)S(1)} %copy-done.12, f32[1024]{0:T(1024)S(1)} %copy-done.9, f32[2560]{0:T(1024)S(1)} %fusion.16, f32[2560]{0:T(1024)S(1)} %broadcast_multiply_fusion), kind=kOutput, calls=%fused_computation.50 | convolution fusion | flops 20061880320 | bytes 45756416 | tf_op jit(solution)/shard_map/nv,nd->vd/dot_general | solution.py:43
  269.6 0.0 copy-start.7
  269.6 116.7 %all-reduce.5.cloned.1.call-done = f32[2560,1024]{0,1:T(8,128)} async-done(((f32[2560,1024]{0,1:T(8,128)}), f32[2560,1024]{0,1:T(8,128)}) %all-reduce.5.cloned.1.call-update) | async-done | bytes 10485776 | tf_op jit(solution)/shard_map/psum | solution.py:45
  386.3 9.1 fusion.19
  395.4 0.0 copy-done.7
  395.5 0.0 copy-start.2
  395.5 0.0 copy-start.11
  395.5 0.0 slice-start
  395.5 9.7 multiply_reduce_fusion
  405.3 0.3 copy-done.2
  405.5 0.0 copy-done.11
  405.5 14.2 %fusion.20 = (f32[1024]{0:T(1024)S(1)}, bf16[2560,1024]{0,1:T(8,128)(2,1)S(1)}) fusion(f32[2560,1024]{0,1:T(8,128)} %get-tuple-element.25, f32[2560]{0:T(1024)S(1)} %negate_multiply_fusion.1, f32[2560]{0:T(1024)S(1)} %multiply_multiply_fusion.6, f32[2560,1024]{0,1:T(8,128)} %copy-done.1, f32[2560]{0:T(1024)S(1)} %broadcast_multiply_fusion, ...), kind=kLoop, calls=%fused_computation.53 | loop fusion | flops 60292096 | bytes 47239168 | tf_op jit(solution)/shard_map/reduce_sum | solution.py:49
  419.7 0.0 copy-start.3
  419.7 2.3 copy-done.3
  422.0 0.0 slice-done
  422.1 0.0 slice-done.1
  422.1 7.4 fusion.11
  429.5 0.0 all-reduce.7.cloned.1.call-update
  429.5 24.2 %psum.78 = f32[2560]{0:T(1024)S(1)} all-reduce(f32[2560]{0:T(1024)S(1)} %get-tuple-element.9), channel_id=1, replica_groups=mesh['dp'=4,'tp'=8] {'tp'}, use_global_device_ids=true, to_apply=%region_7.8 | all-reduce | flops 2560 | bytes 20480 | tf_op jit(solution)/shard_map/psum | solution.py:35
  453.7 0.6 multiply_reduce_fusion.3
  454.3 23.3 %all-reduce = (f32[]{:T(128)}, f32[1024]{0:T(1024)}, f32[1024]{0:T(1024)}, f32[1024]{0:T(1024)}, f32[3824]{0:T(1024)}) all-reduce(f32[]{:T(128)} %multiply_reduce_fusion.3, f32[1024]{0:T(1024)S(1)} %get-tuple-element.21, f32[1024]{0:T(1024)S(1)} %get-tuple-element.10, ...), channel_id=1, replica_groups=mesh['dp'=4,'tp'=8] {'dp'}, use_global_device_ids=true, to_apply=%region_9.10 | all-reduce | flops 6897 | bytes 55176 | tf_op jit(solution)/shard_map/psum | solution.py:39
  478.3 10.0 convolution_convert_fusion.1
  488.3 9.0 reshape.77
  497.3 0.0 copy-done.5
  497.3 22.6 %convolution_convert_fusion = bf16[128,128,1024]{2,1,0:T(8,128)(2,1)} fusion(bf16[128,20,1024]{2,1,0:T(8,128)(2,1)} %reshape.77, s32[128,20]{1,0:T(8,128)S(1)} %copy-done.5), kind=kOutput, calls=%fused_computation.7 | convolution fusion | flops 688193536 | bytes 38807552 | tf_op jit(solution)/shard_map/bps,bpd->bsd/dot_general | solution.py:53
  519.9 569.5 %all-reduce.7.cloned.1.call-done = (f32[1024,1024]{1,0:T(8,128)}, f32[3824,1024]{1,0:T(8,128)}) async-done(((f32[1024,1024]{1,0:T(8,128)}, f32[3824,1024]{1,0:T(8,128)}), (f32[1024,1024]{1,0:T(8,128)}, f32[3824,1024]{1,0:T(8,128)})) %all-reduce.7.cloned.1.call-update) | async-done | bytes 19857424 | tf_op jit(solution)/shard_map/psum | solution.py:48
  1089.4 4.8 copy.28
  1094.2 14.8 %copy.29 = f32[3824,1024]{1,0:T(8,128)} copy(f32[3824,1024]{1,0:T(8,128)} %get-tuple-element.38) | data formatting | bytes 31326208
  (10 shorter events, 0.0 us)
Async XLA Ops:
  7.2 43.0 %copy-start = (bf16[1024,1024]{1,0:T(8,128)(2,1)S(1)}, bf16[1024,1024]{1,0:T(8,128)(2,1)}, u32[]{:S(2)}) copy-start(bf16[1024,1024]{1,0:T(8,128)(2,1)} %param.14) | copy-start | bytes 6291460
  7.2 379.1 %all-reduce.5.cloned.1.call-start = ((), (), s32[]{:S(2)}) async-start(), calls=%async_computation | async-start | bytes 20971520 | tf_op jit(solution)/shard_map/psum | solution.py:45
  25.4 15.8 %copy-start.4 = (s32[128,20]{1,0:T(8,128)}, s32[128,20]{1,0:T(8,128)S(1)}, u32[]{:S(2)}) copy-start(s32[128,20]{1,0:T(8,128)S(1)} %copy.21) | copy-start | bytes 30724
  41.2 9.0 copy-start.10
  82.7 38.0 %copy-start.1 = (f32[2560,1024]{0,1:T(8,128)}, f32[2560,1024]{0,1:T(8,128)S(1)}, u32[]{:S(2)}) copy-start(f32[2560,1024]{0,1:T(8,128)S(1)} %get-tuple-element.24) | copy-start | bytes 31457284
  82.7 1.1 copy-start.8
  82.7 1.1 copy-start.9
  82.7 1.2 copy-start.12
  83.8 36.9 %copy-start.6 = (f32[2560]{0:T(1024)}, f32[2560]{0:T(1024)S(1)}, u32[]{:S(2)}) copy-start(f32[2560]{0:T(1024)S(1)} %multiply_reduce_fusion.2) | copy-start | bytes 30724
  240.2 849.2 %all-reduce.7.cloned.1.call-start = ((), (), s32[]{:S(2)}) async-start(), calls=%async_computation.1 | async-start | bytes 39714816 | tf_op jit(solution)/shard_map/psum | solution.py:48
  269.6 125.8 %copy-start.7 = (f32[2560]{0:T(1024)S(1)}, f32[2560]{0:T(1024)}, u32[]{:S(2)}) copy-start(f32[2560]{0:T(1024)} %copy-done.6) | copy-start | bytes 30724
  395.5 10.0 copy-start.2
  395.5 10.0 copy-start.11
  395.5 26.6 %slice-start = ((s8[5242880]{0:T(1024)(128)(4,1)}), s8[4194304]{0:T(1024)(128)(4,1)S(1)}, s32[]{:S(2)}) async-start(s8[5242880]{0:T(1024)(128)(4,1)} %bitcast.12), calls=%async_computation.2 | async-start | bytes 8388608
  405.5 16.5 %slice-start.1 = ((s8[5242880]{0:T(1024)(128)(4,1)}), s8[1048576]{0:T(1024)(128)(4,1)S(1)}, s32[]{:S(2)}) async-start(s8[5242880]{0:T(1024)(128)(4,1)} %bitcast.12), calls=%async_computation.3 | async-start | bytes 2097152
  419.7 2.4 copy-start.3
  488.3 9.0 copy-start.5
Sparse Core Ops, SparseCore 0:
  240.3 145.9 all-reduce.4
  429.6 659.7 all-reduce.6
where the time goes:
time: 1120 us
  waiting for transfers between devices  686 us (61%)
  matrix products  182 us (16%)
  blocking collectives  106 us (9%)
  other arithmetic  83.6 us (7%)
  local copies, waits for them, and re-layouts  42.3 us (4%)
  between operations  17.1 us (2%)
    psum x1, waiting for transfers between devices, local_step(): lax.psum(jnp.einsum('nd,ne->de', tok_rows, d_pre_bf, preferred_element_ty...  569 us
    psum x1, waiting for transfers between devices, local_step(): lax.psum(jnp.einsum('nv,vd->nd', dz_bf, embed, preferred_element_type=jnp...  117 us
    dot_general x1, matrix products, local_step(): jnp.einsum('nd,vd->nv', t_bf, embed, preferred_element_type=jnp.float32)  36.9 us
    dot_general x1, matrix products, local_step(): pre_act = jnp.dot(tok_rows, w_t, preferred_element_type=jnp.float32) + b_t  32.5 us
    reduce_sum x1, other arithmetic, local_step(): d_out_bias = lax.psum(jnp.sum(d_logits, axis=0), 'dp')  30.2 us
    dot_general x1, matrix products, local_step(): jnp.einsum('nv,nd->vd', dz_bf, t_bf, preferred_element_type=jnp.float32)  29.4 us
    dot_general x1, matrix products, local_step(): jnp.einsum('nv,vd->nd', dz_bf, embed, preferred_element_type=jnp.float32)  27.2 us
    psum x1, blocking collectives, local_step(): lax.psum(jnp.sum(jnp.where(lab_hot, logits, 0.0), axis=1), 'tp')  24.2 us
  transfers between devices with their start and end apart: 2, of which 2 were waited for; matrix products, arithmetic and copies ran while one was open for 6% of the time, Pallas kernels for 0%

commit v1 on v0

v1 whole, which is shorter than its diff:
```python
import functools

import jax
import jax.numpy as jnp
from jax import lax
from jax.experimental import pallas as pl
from jax.experimental.pallas import tpu as pltpu
from jax.sharding import PartitionSpec as P

LN_EPS = 1e-12
LOSS_EPS = 1e-5
VMEM_LIMIT = 60 * 1024 * 1024
ROW_CHUNK = 512
BLOCK_N = 512
GROUP = 8


def gelu_norm(pre_act, gamma, beta):
    activated = jax.nn.gelu(pre_act, approximate=False)
    mean_val = jnp.mean(activated, axis=-1, keepdims=True)
    centered = activated - mean_val
    variance = jnp.mean(centered * centered, axis=-1, keepdims=True)
    return centered * lax.rsqrt(variance + LN_EPS) * gamma + beta


def row_chunks(rows):
    return [(start, min(ROW_CHUNK, rows - start)) for start in range(0, rows, ROW_CHUNK)]


def params(**kw):
    return pltpu.CompilerParams(vmem_limit_bytes=VMEM_LIMIT, **kw)


def pick_kernel(rowpos_ref, hid_ref, out_ref):
    rows, depth = out_ref.shape[0], hid_ref.shape[0]
    hot = (rowpos_ref[...] == lax.broadcasted_iota(jnp.int32, (rows, depth), 1)).astype(jnp.bfloat16)
    out_ref[...] = jnp.dot(hot, hid_ref[...], preferred_element_type=jnp.float32).astype(jnp.bfloat16)


def pick(hidden, rowpos):
    groups = hidden.shape[0] // GROUP
    depth = GROUP * hidden.shape[1]
    width = hidden.shape[2]
    rows = rowpos.shape[0] // groups
    return pl.pallas_call(
        pick_kernel,
        grid=(groups,),
        in_specs=[pl.BlockSpec((rows, 1), lambda g: (g, 0)), pl.BlockSpec((depth, width), lambda g: (g, 0))],
        out_specs=pl.BlockSpec((rows, width), lambda g: (g, 0)),
        out_shape=jax.ShapeDtypeStruct((rows * groups, width), jnp.bfloat16),
        compiler_params=params(),
        cost_estimate=pl.CostEstimate(flops=2 * rows * groups * depth * width, bytes_accessed=hidden.size * 2, transcendentals=0),
        name="pick",
    )(rowpos.reshape(-1, 1), hidden.reshape(groups * depth, width))


def put_kernel(rowpos_ref, dh_ref, out_ref):
    depth, rows = out_ref.shape[0], dh_ref.shape[0]
    hot = (rowpos_ref[0] == lax.broadcasted_iota(jnp.int32, (depth, rows), 0)).astype(jnp.bfloat16)
    out_ref[...] = jnp.dot(hot, dh_ref[...].astype(jnp.bfloat16), preferred_element_type=jnp.float32).astype(jnp.bfloat16)


def put(d_rows, rowpos, batch, seq_len):
    groups = batch // GROUP
    depth = GROUP * seq_len
    width = d_rows.shape[1]
    rows = rowpos.shape[0] // groups
    out = pl.pallas_call(
        put_kernel,
        grid=(groups,),
        in_specs=[pl.BlockSpec((1, 1, rows), lambda g: (g, 0, 0)), pl.BlockSpec((rows, width), lambda g: (g, 0))],
        out_specs=pl.BlockSpec((depth, width), lambda g: (g, 0)),
        out_shape=jax.ShapeDtypeStruct((groups * depth, width), jnp.bfloat16),
        compiler_params=params(),
        cost_estimate=pl.CostEstimate(flops=2 * rows * groups * depth * width, bytes_accessed=groups * depth * width * 2, transcendentals=0),
        name="put",
    )(rowpos.reshape(groups, 1, rows), d_rows)
    return out.reshape(batch, seq_len, width)


def logits_kernel(which_ref, t_ref, embed_ref, bias_ref, lab_ref, z_ref, stat_ref):
    del which_ref
    t_blk = t_ref[...].astype(jnp.bfloat16)
    lab = lab_ref[...]
    cols = t_blk.shape[0]
    top = jnp.full((1, cols), -jnp.inf, jnp.float32)
    total = jnp.zeros((1, cols), jnp.float32)
    target = jnp.zeros((1, cols), jnp.float32)
    for start, rows in row_chunks(embed_ref.shape[0]):
        z = lax.dot_general(embed_ref[start:start + rows, :], t_blk, (((1,), (1,)), ((), ())), preferred_element_type=jnp.float32)
        z = z + bias_ref[start:start + rows, :]
        z_ref[start:start + rows, :] = z
        new_top = jnp.maximum(top, jnp.max(z, axis=0, keepdims=True))
        total = total * jnp.exp(top - new_top) + jnp.sum(jnp.exp(z - new_top), axis=0, keepdims=True)
        top = new_top
        hot = lab == lax.broadcasted_iota(jnp.int32, (rows, cols), 0) + start
        target = target + jnp.sum(jnp.where(hot, z, 0.0), axis=0, keepdims=True)
    stat_ref[0:1, :] = top
    stat_ref[1:2, :] = total
    stat_ref[2:3, :] = target
    stat_ref[3:8, :] = jnp.zeros((5, cols), jnp.float32)


def block_map(planes, per_plane):
    if planes == 0:
        return lambda k, which: k
    return lambda k, which: lax.rem(which[0] + 1 + k // per_plane, planes) * per_plane + lax.rem(k, per_plane)


def logits_call(which, t_rows, embed, bias_col, lab_row, planes, per_plane):
    slots = lab_row.shape[1]
    vocab, width = embed.shape
    where = block_map(planes, per_plane)
    return pl.pallas_call(
        logits_kernel,
        grid_spec=pltpu.PrefetchScalarGridSpec(
            num_scalar_prefetch=1,
            grid=(slots // BLOCK_N,),
            in_specs=[
                pl.BlockSpec((BLOCK_N, width), lambda k, which: (where(k, which), 0)),
                pl.BlockSpec((vocab, width), lambda k, which: (0, 0), pipeline_mode=pl.Buffered(1)),
                pl.BlockSpec((vocab, 1), lambda k, which: (0, 0), pipeline_mode=pl.Buffered(1)),
                pl.BlockSpec((1, BLOCK_N), lambda k, which: (0, k)),
            ],
            out_specs=[
                pl.BlockSpec((vocab, BLOCK_N), lambda k, which: (0, k)),
                pl.BlockSpec((8, BLOCK_N), lambda k, which: (0, k)),
            ],
        ),
        out_shape=[jax.ShapeDtypeStruct((vocab, slots), jnp.float32), jax.ShapeDtypeStruct((8, slots), jnp.float32)],
        compiler_params=params(),
        cost_estimate=pl.CostEstimate(flops=2 * slots * vocab * width, bytes_accessed=slots * vocab * 4, transcendentals=slots * vocab),
        name="logits",
    )(which, t_rows, embed, bias_col, lab_row)


def dz_of(z, stat_ref, lab, start):
    soft = jnp.exp(z - stat_ref[0:1, :]) * stat_ref[1:2, :]
    hot = lab == lax.broadcasted_iota(jnp.int32, z.shape, 0) + start
    return jnp.where(hot, soft - 1.0, soft) * stat_ref[2:3, :]


def dt_kernel(z_ref, stat_ref, lab_ref, embed_ref, dt_ref):
    lab = lab_ref[...]
    acc = None
    for start, rows in row_chunks(embed_ref.shape[0]):
        dz = dz_of(z_ref[start:start + rows, :], stat_ref, lab, start).astype(jnp.bfloat16)
        part = lax.dot_general(dz, embed_ref[start:start + rows, :], (((0,), (0,)), ((), ())), preferred_element_type=jnp.float32)
        acc = part if acc is None else acc + part
    dt_ref[...] = acc


def dt_call(z, stat, lab_row, embed):
    slots = z.shape[1]
    vocab, width = embed.shape
    block = 256
    return pl.pallas_call(
        dt_kernel,
        grid=(slots // block,),
        in_specs=[
            pl.BlockSpec((vocab, block), lambda k: (0, k)),
            pl.BlockSpec((8, block), lambda k: (0, k)),
            pl.BlockSpec((1, block), lambda k: (0, k)),
            pl.BlockSpec((vocab, width), lambda k: (0, 0), pipeline_mode=pl.Buffered(1)),
        ],
        out_specs=pl.BlockSpec((block, width), lambda k: (k, 0)),
        out_shape=jax.ShapeDtypeStruct((slots, width), jnp.float32),
        compiler_params=params(),
        cost_estimate=pl.CostEstimate(flops=2 * slots * vocab * width, bytes_accessed=slots * vocab * 4, transcendentals=slots * vocab),
        name="dt",
    )(z, stat, lab_row, embed)


def de_kernel(first, which_ref, z_ref, stat_ref, lab_ref, t_ref, *rest):
    del which_ref
    if first:
        de_ref, db_ref = rest
    else:
        de_in, db_in, de_ref, db_ref, sems = rest
    k = pl.program_id(0)

    @pl.when(k == 0)
    def _():
        if first:
            de_ref[...] = jnp.zeros_like(de_ref)
            db_ref[...] = jnp.zeros_like(db_ref)
        else:
            one = pltpu.make_async_copy(de_in, de_ref, sems.at[0])
            two = pltpu.make_async_copy(db_in, db_ref, sems.at[1])
            one.start()
            two.start()
            one.wait()
            two.wait()

    lab = lab_ref[...]
    t_blk = t_ref[...].astype(jnp.bfloat16)
    for start, rows in row_chunks(z_ref.shape[0]):
        dz = dz_of(z_ref[start:start + rows, :], stat_ref, lab, start)
        lanes = dz[:, 0:128]
        for c in range(128, dz.shape[1], 128):
            lanes = lanes + dz[:, c:c + 128]
        db_ref[start:start + rows, :] += lanes
        de_ref[start:start + rows, :] += jnp.dot(dz.astype(jnp.bfloat16), t_blk, preferred_element_type=jnp.float32)


def de_call(which, z, stat, lab_row, t_rows, planes, per_plane, carry=None):
    vocab, slots = z.shape
    width = t_rows.shape[1]
    where = block_map(planes, per_plane)
    first = carry is None
    in_specs = [
        pl.BlockSpec((vocab, BLOCK_N), lambda k, which: (0, k)),
        pl.BlockSpec((8, BLOCK_N), lambda k, which: (0, k)),
        pl.BlockSpec((1, BLOCK_N), lambda k, which: (0, k)),
        pl.BlockSpec((BLOCK_N, width), lambda k, which: (where(k, which), 0)),
    ]
    args = [which, z, stat, lab_row, t_rows]
    scratch = []
    if not first:
        in_specs += [pl.BlockSpec(memory_space=pl.ANY), pl.BlockSpec(memory_space=pl.ANY)]
        args += list(carry)
        scratch = [pltpu.SemaphoreType.DMA((2,))]
    return pl.pallas_call(
        functools.partial(de_kernel, first),
        grid_spec=pltpu.PrefetchScalarGridSpec(
            num_scalar_prefetch=1,
            grid=(slots // BLOCK_N,),
            in_specs=in_specs,
            out_specs=[
                pl.BlockSpec((vocab, width), lambda k, which: (0, 0), pipeline_mode=pl.Buffered(1)),
                pl.BlockSpec((vocab, 128), lambda k, which: (0, 0), pipeline_mode=pl.Buffered(1)),
            ],
            scratch_shapes=scratch,
        ),
        out_shape=[jax.ShapeDtypeStruct((vocab, width), jnp.float32), jax.ShapeDtypeStruct((vocab, 128), jnp.float32)],
        compiler_params=params(),
        cost_estimate=pl.CostEstimate(flops=2 * slots * vocab * width, bytes_accessed=slots * vocab * 4, transcendentals=slots * vocab),
        name="de",
    )(*args)


def combine(stat, weights_row, denom):
    parts = lax.all_gather(stat[:3], "tp", axis=0)
    top = jnp.max(parts[:, 0], axis=0)
    total = jnp.sum(parts[:, 1] * jnp.exp(parts[:, 0] - top[None]), axis=0)
    target = jnp.sum(parts[:, 2], axis=0)
    zero = jnp.zeros_like(top)
    rows = jnp.stack([top, 1.0 / total, weights_row / denom, zero, zero, zero, zero, zero])
    return rows, jnp.log(total) + top - target


def solution(mesh):
    dp, tp = mesh.shape["dp"], mesh.shape["tp"]

    def local_step(hidden, positions, labels, weights, w_t, b_t, gamma, beta, embed, out_bias):
        batch, seq_len, width = hidden.shape
        max_pred = positions.shape[1]
        shard_vocab = embed.shape[0]
        slots = batch * max_pred
        share = slots // tp
        per_plane = slots // BLOCK_N
        dp_idx, tp_idx = lax.axis_index("dp"), lax.axis_index("tp")
        which = dp_idx.reshape(1).astype(jnp.int32)

        small = jnp.stack([labels.reshape(-1).astype(jnp.float32), weights.reshape(-1)])
        small = lax.all_gather(small, "dp", axis=0)
        denom = jnp.sum(small[:, 1]) + LOSS_EPS
        ring = lax.dynamic_slice_in_dim(jnp.concatenate([small, small]), dp_idx + 1, dp - 1, 0)
        far_lab = (ring[:, 0].reshape(1, -1)).astype(jnp.int32) - tp_idx * shard_vocab
        far_w = ring[:, 1].reshape(-1)
        own_lab = labels.reshape(1, -1) - tp_idx * shard_vocab
        own_w = weights.reshape(-1)

        rowpos = (positions + (jnp.arange(batch, dtype=jnp.int32) % GROUP * seq_len)[:, None]).reshape(-1)
        bias_col = out_bias.reshape(-1, 1)

        tok_rows = pick(hidden, rowpos)
        normed = gelu_norm(jnp.dot(tok_rows, w_t, preferred_element_type=jnp.float32) + b_t, gamma, beta)
        t_own = normed.astype(jnp.bfloat16)
        t_part = lax.dynamic_slice_in_dim(t_own, tp_idx * share, share, 0)
        t_part = lax.optimization_barrier(t_part.astype(jnp.float32))
        t_all = lax.all_gather(t_part, ("dp", "tp"), axis=0, tiled=True)

        z_own, stat_own = logits_call(which, t_own, embed, bias_col, own_lab, 0, per_plane)
        rows_own, ce = combine(stat_own, own_w, denom)
        dt_part = dt_call(z_own, rows_own, own_lab, embed)
        carry = de_call(which, z_own, rows_own, own_lab, t_own, 0, per_plane)
        loss = jnp.sum(own_w * ce)

        t_all, carry, dt_part = lax.optimization_barrier((t_all, carry, dt_part))
        d_normed = lax.psum_scatter(dt_part, "tp", scatter_dimension=0, tiled=True)
        z_far, stat_far = logits_call(which, t_all, embed, bias_col, far_lab, dp, per_plane)
        rows_far, _ = combine(stat_far, far_w, denom)
        d_embed, d_bias = de_call(which, z_far, rows_far, far_lab, t_all, dp, per_plane, carry)
        d_out_bias = jnp.sum(d_bias, axis=1)

        part_rows = lax.dynamic_slice_in_dim(tok_rows, tp_idx * share, share, 0)
        pre_act = jnp.dot(part_rows, w_t, preferred_element_type=jnp.float32) + b_t
        _, norm_vjp = jax.vjp(gelu_norm, pre_act, gamma, beta)
        d_pre, d_gamma, d_beta = norm_vjp(d_normed)
        d_pre_bf = d_pre.astype(jnp.bfloat16)
        d_rows = jnp.einsum("ne,de->nd", d_pre_bf, w_t, preferred_element_type=jnp.float32).astype(jnp.bfloat16)
        d_rows = lax.optimization_barrier(d_rows.astype(jnp.float32))
        d_rows = lax.all_gather(d_rows, "tp", axis=0, tiled=True)
        d_w_t = jnp.einsum("nd,ne->de", part_rows, d_pre_bf, preferred_element_type=jnp.float32)
        d_b_t = jnp.sum(d_pre, axis=0)
        loss = jnp.where(tp_idx == 0, loss, 0.0)
        vecs = jnp.stack([d_b_t, d_gamma, d_beta, jnp.full_like(d_b_t, loss)])
        d_w_t, vecs = lax.psum((d_w_t, vecs), ("dp", "tp"))
        d_hidden = put(d_rows, rowpos, batch, seq_len)
        return vecs[3, 0] / denom, d_hidden, d_w_t, vecs[0], vecs[1], vecs[2], d_embed, d_out_bias

    in_specs = (P("dp", None, None), P("dp", None), P("dp", None), P("dp", None), P(None, None), P(None), P(None), P(None), P("tp", None), P("tp"))
    out_specs = (P(), P("dp", None, None), P(None, None), P(None), P(None), P(None), P("tp", None), P("tp"))
    return jax.shard_map(local_step, mesh=mesh, in_specs=in_specs, out_specs=out_specs, check_vma=False)
```

time: 1120 us -> 693 us (0.62)
  waiting for transfers between devices: 686 us -> 179 us
  Pallas kernels: 0 us -> 326 us
  matrix products: 182 us -> 42.5 us
  other arithmetic: 83.6 us -> 20.3 us
  blocking collectives: 106 us -> 75.9 us
  local copies, waits for them, and re-layouts: 42.3 us -> 22.6 us
    psum x2 -> x1, waiting for transfers between devices: 686 us -> 0.01 us  [local_step(): d_w_t, vecs = lax.psum((d_w_t, vecs), ('dp', 'tp'))]
    pallas_call x0 -> x7, Pallas kernels: none -> 326 us  [the longest x2 127 us: de_call(): pl.pallas_call(functools.partial(de_kernel, first), grid_spec=pltpu.Prefe...]
    dot_general x7 -> x3, matrix products: 172 us -> 40.6 us  [the longest x1 30.2 us: local_step(): jnp.dot(tok_rows, w_t, preferred_element_type=jnp.float32) + b_t]
    all_gather x0 -> x2, waiting for transfers between devices: none -> 103 us  [the longest x1 103 us: local_step(): t_all = lax.all_gather(t_part, ('dp', 'tp'), axis=0, tiled=True)]
    reduce_scatter x0 -> x1, waiting for transfers between devices: none -> 76.8 us  [local_step(): d_normed = lax.psum_scatter(dt_part, 'tp', scatter_dimension=0, tiled=True)]
    reduce_sum x5 -> x7, other arithmetic: 62.9 us -> 6.96 us  [the longest x1 2.74 us: local_step(): d_out_bias = jnp.sum(d_bias, axis=1)]
    psum x4 -> x1, blocking collectives: 84 us -> 39.7 us  [local_step(): d_w_t, vecs = lax.psum((d_w_t, vecs), ('dp', 'tp'))]
    all_gather x0 -> x3, blocking collectives: none -> 36.1 us  [the longest x2 22 us: combine(): parts = lax.all_gather(stat[:3], 'tp', axis=0)]
  transfers between devices with their start and end apart: 2 -> 4, of which waited for: 2 -> 2; matrix products, arithmetic and copies ran while one was open for 6% -> 4% of each run, Pallas kernels for 0% -> 45%
where the time goes in v1:
time: 693 us; the launch traced here: 685 us
  Pallas kernels  326 us (47%)
  waiting for transfers between devices  179 us (26%)
  blocking collectives  75.9 us (11%)
  matrix products  42.5 us (6%)
  local copies, waits for them, and re-layouts  22.6 us (3%)
  other arithmetic  20.3 us (3%)
  between operations  17.6 us (3%)
    pallas_call x2, Pallas kernels, de_call(): pl.pallas_call(functools.partial(de_kernel, first), grid_spec=pltpu.Prefe...  127 us
    pallas_call x2, Pallas kernels, logits_call(): pl.pallas_call(logits_kernel, grid_spec=pltpu.PrefetchScalarGridSpec(num_...  125 us
    all_gather x1, waiting for transfers between devices, local_step(): t_all = lax.all_gather(t_part, ('dp', 'tp'), axis=0, tiled=True)  103 us
    reduce_scatter x1, waiting for transfers between devices, local_step(): d_normed = lax.psum_scatter(dt_part, 'tp', scatter_dimension=0, tiled=True)  76.8 us
    psum x1, blocking collectives, local_step(): d_w_t, vecs = lax.psum((d_w_t, vecs), ('dp', 'tp'))  39.7 us
    pallas_call x1, Pallas kernels, dt_call(): pl.pallas_call(dt_kernel, grid=(slots // block,), in_specs=[pl.BlockSpec(...  31.3 us
    dot_general x1, matrix products, local_step(): jnp.dot(tok_rows, w_t, preferred_element_type=jnp.float32) + b_t  30.2 us
    all_gather x2, blocking collectives, combine(): parts = lax.all_gather(stat[:3], 'tp', axis=0)  22 us
  transfers between devices with their start and end apart: 4, of which 2 were waited for; matrix products, arithmetic and copies ran while one was open for 4% of the time, Pallas kernels for 45%

profile of v1, /device:TPU:0, one launch (start us, length us, event | category | flops | bytes accessed | tf_op | source)
XLA Modules:
  0.0 685.5 jit_solution(13381882955125685786)
XLA Ops:
  7.2 0.0 all-gather.9.cloned.1.call-start
  7.2 0.8 broadcast_add_fusion
  8.1 0.1 copy.37
  8.2 1.5 reshape_reshape.8.rowpos_ref
  9.7 21.1 %pick.1 = bf16[2560,1024]{1,0:T(8,128)(2,1)} custom-call(s32[2560,1]{1,0:T(8,128)} %reshape_reshape.8.rowpos_ref, bf16[16384,1024]{1,0:T(8,128)(2,1)} %bitcast.49), custom_call_target="tpu_custom_call" | custom-call | flops 5368709120 | bytes 33554432 | tf_op jit(solution)/shard_map/pick/pallas_call | solution.py:45
  30.7 30.2 %fusion.42 = (f32[2560]{0:T(1024)S(1)}, f32[2560,1024]{1,0:T(8,128)S(1)}) fusion(f32[1024]{0:T(1024)S(1)} %copy-done.22, bf16[2560,1024]{1,0:T(8,128)(2,1)} %pick.1, bf16[1024,1024]{1,0:T(8,128)(2,1)S(1)} %copy-done), kind=kOutput, calls=%fused_computation.99 | convolution fusion | flops 5541721600 | bytes 17840128 | tf_op jit(solution)/shard_map/dot_general | solution.py:278
  61.0 1.2 multiply_reduce_fusion
  62.3 2.8 copy-done.2
  65.1 5.4 add_convert_fusion.t_ref
  70.6 2.4 copy-done.4
  72.9 1.2 dynamic-slice_convert_fusion
  74.2 0.6 reduce-scatter.2.cloned.1.call-start
  74.8 0.1 copy.39
  74.9 0.7 sub.59.lab_ref
  75.6 1.8 reshape.203.bias_ref
  77.4 34.9 %logits.2 = (f32[3824,2560]{1,0:T(8,128)}, f32[8,2560]{1,0:T(8,128)}) custom-call(s32[1]{0:T(128)} %bitcast.1.which_ref, bf16[2560,1024]{1,0:T(8,128)(2,1)} %copy-done.4, bf16[3824,1024]{1,0:T(8,128)(2,1)} %embed_ref.5, f32[3824,1]{1,0:T(8,128)} %reshape.203.bias_ref, s32[1,2560]{1,0:T(1,128)} %sub.59.lab_ref), custom_call_target="tpu_custom_call" | custom-call | flops 20048773120 | bytes 39157760 | tf_op jit(solution)/shard_map/logits/pallas_call | solution.py:114
  112.3 0.9 slice_bitcast_fusion.1
  113.2 10.9 %all-gather.3 = f32[8,3,2560]{2,1,0:T(4,128)S(1)} all-gather(f32[1,3,2560]{2,1,0:T(4,128)S(1)} %slice_bitcast_fusion.1), channel_id=2, replica_groups=mesh['dp'=4,'tp'=8] {'tp'}, dimensions={0}, use_global_device_ids=true | all-gather | bytes 276480 | tf_op jit(solution)/shard_map/all_gather | solution.py:243
  124.1 0.2 fusion.39
  124.4 0.6 add_subtract_fusion
  125.1 0.1 copy.43
  125.2 0.1 convert_element_type.43
  125.3 0.1 copy.42
  125.4 0.1 reshape.187
  125.6 14.2 %all-gather.4 = f32[4,2,2560]{2,1,0:T(2,128)S(1)} all-gather(f32[1,2,2560]{2,1,0:T(2,128)S(1)} %maximum_bitcast_fusion), channel_id=3, replica_groups=mesh['dp'=4,'tp'=8] {'dp'}, dimensions={0}, use_global_device_ids=true | all-gather | bytes 102400 | tf_op jit(solution)/shard_map/all_gather | solution.py:266
  139.7 0.7 slice_reduce_fusion.1
  141.1 0.7 stack.37.stat_ref
  141.8 31.3 %dt.1 = f32[2560,1024]{1,0:T(8,128)} custom-call(f32[3824,2560]{1,0:T(8,128)} %get-tuple-element.20.z_ref, f32[8,2560]{1,0:T(8,128)} %stack.37.stat_ref, s32[1,2560]{1,0:T(1,128)} %sub.59.lab_ref, bf16[3824,1024]{1,0:T(8,128)(2,1)} %embed_ref.5), custom_call_target="tpu_custom_call" | custom-call | flops 20048773120 | bytes 39157760 | tf_op jit(solution)/shard_map/dt/pallas_call | solution.py:157
  173.2 35.2 %de.2 = (f32[3824,1024]{1,0:T(8,128)}, f32[3824,128]{1,0:T(8,128)}) custom-call(s32[1]{0:T(128)} %bitcast.1.which_ref, f32[3824,2560]{1,0:T(8,128)} %get-tuple-element.20.z_ref, f32[8,2560]{1,0:T(8,128)} %stack.37.stat_ref, s32[1,2560]{1,0:T(1,128)} %sub.59.lab_ref, bf16[2560,1024]{1,0:T(8,128)(2,1)} %copy-done.4), custom_call_target="tpu_custom_call" | custom-call | flops 20048773120 | bytes 39157760 | tf_op jit(solution)/shard_map/de/pallas_call | solution.py:223
  208.4 102.6 %all-gather.9.cloned.1.call-done.t_ref = f32[10240,1024]{1,0:T(8,128)} async-done(((f32[320,1024]{1,0:T(8,128)}), f32[10240,1024]{1,0:T(8,128)}) %all-gather.9.cloned.1.call-update) | async-done | bytes 41943056 | tf_op jit(solution)/shard_map/all_gather | solution.py:282
  311.0 0.3 all-gather.11.cloned.1.call-start
  311.3 6.0 fusion.36
  317.2 0.6 broadcast_multiply_fusion.1
  317.8 76.8 %reduce-scatter.2.cloned.1.call-done = f32[320,1024]{1,0:T(8,128)} async-done(((f32[2560,1024]{1,0:T(8,128)}), f32[320,1024]{1,0:T(8,128)}) %reduce-scatter.2.cloned.1.call-update) | async-done | bytes 1310736 | tf_op jit(solution)/shard_map/reduce_scatter | solution.py:291
  394.6 1.9 multiply_reduce_fusion.2
  396.5 1.2 fusion.16
  397.7 0.1 copy-done.7
  397.8 0.4 copy-done.8
  398.2 1.6 fusion.35
  399.8 0.8 copy-done.5
  400.6 1.9 fusion.9
  402.5 0.0 all-reduce.2.cloned.1.call-start
  402.6 0.8 copy-done.10
  403.4 0.7 reshape_reshape.9.rowpos_ref
  404.1 0.1 sub.65
  404.2 0.6 multiply_reduce_fusion.4
  405.4 0.1 pad.5.clone
  405.5 0.1 fusion.29
  405.6 0.6 fusion.30
  406.3 90.4 %logits.3 = (f32[3824,7680]{1,0:T(8,128)}, f32[8,7680]{1,0:T(8,128)}) custom-call(s32[1]{0:T(128)} %bitcast.1.which_ref, f32[10240,1024]{1,0:T(8,128)} %all-gather.9.cloned.1.call-done.t_ref, bf16[3824,1024]{1,0:T(8,128)(2,1)} %embed_ref.5, f32[3824,1]{1,0:T(8,128)} %reshape.203.bias_ref, s32[1,7680]{1,0:T(1,128)} %bitcast.52), custom_call_target="tpu_custom_call" | custom-call | flops 60146319360 | bytes 117473280 | tf_op jit(solution)/shard_map/logits/pallas_call | solution.py:114
  496.7 1.0 slice_bitcast_fusion
  497.7 11.0 %all-gather.5 = f32[8,3,7680]{2,1,0:T(4,128)S(1)} all-gather(f32[1,3,7680]{2,1,0:T(4,128)S(1)} %slice_bitcast_fusion), channel_id=4, replica_groups=mesh['dp'=4,'tp'=8] {'tp'}, dimensions={0}, use_global_device_ids=true | all-gather | bytes 829440 | tf_op jit(solution)/shard_map/all_gather | solution.py:243
  508.7 0.5 fusion.38
  509.2 0.1 fusion.23
  509.4 0.9 stack.42.stat_ref
  510.3 4.4 fusion.17
  514.7 92.2 %de.3 = (f32[3824,1024]{1,0:T(8,128)}, f32[3824,128]{1,0:T(8,128)}) custom-call(s32[1]{0:T(128)} %bitcast.1.which_ref, f32[3824,7680]{1,0:T(8,128)} %get-tuple-element.26.z_ref, f32[8,7680]{1,0:T(8,128)} %stack.42.stat_ref, s32[1,7680]{1,0:T(1,128)} %bitcast.53, f32[10240,1024]{1,0:T(8,128)} %all-gather.9.cloned.1.call-done.t_ref, ...), custom_call_target="tpu_custom_call" | custom-call | flops 60146319360 | bytes 117473280 | tf_op jit(solution)/shard_map/de/pallas_call | solution.py:223
  607.0 2.7 reduce_sum.165
  609.7 0.1 maximum_maximum_fusion
  609.8 39.7 %psum.14 = f32[4,1024]{1,0:T(4,128)S(1)} all-reduce(f32[4,1024]{1,0:T(4,128)S(1)} %maximum_maximum_fusion), channel_id=1, replica_groups=mesh['dp'=4,'tp'=8] {'dp','tp'}, use_global_device_ids=true, to_apply=%region_15.16 | all-reduce | flops 4096 | bytes 32768 | tf_op jit(solution)/shard_map/psum | solution.py:309
  649.5 0.5 slice.62
  650.7 0.6 fusion.40
  651.3 21.1 %put.1 = bf16[16384,1024]{1,0:T(8,128)(2,1)} custom-call(s32[16,1,160]{2,1,0:T(1,128)} %reshape_reshape.9.rowpos_ref, f32[2560,1024]{1,0:T(8,128)} %all-gather.11.cloned.1.call-done.dh_ref), custom_call_target="tpu_custom_call" | custom-call | flops 5368709120 | bytes 33554432 | tf_op jit(solution)/shard_map/put/pallas_call | solution.py:68
  672.4 4.9 copy.71
  (65 shorter events, 0.4 us)
Async XLA Ops:
  7.2 23.6 %copy-start = (bf16[1024,1024]{1,0:T(8,128)(2,1)S(1)}, bf16[1024,1024]{1,0:T(8,128)(2,1)}, u32[]{:S(2)}) copy-start(bf16[1024,1024]{1,0:T(8,128)(2,1)} %param.14) | copy-start | bytes 6291460
  7.2 303.8 %all-gather.9.cloned.1.call-start = ((), (), s32[]{:S(2)}) async-start(), calls=%async_computation.1 | async-start | bytes 43253760 | tf_op jit(solution)/shard_map/all_gather | solution.py:282
  8.2 22.5 %copy-start.9 = (s32[128,20]{1,0:T(8,128)}, s32[128,20]{1,0:T(8,128)S(1)}, u32[]{:S(2)}) copy-start(s32[128,20]{1,0:T(8,128)S(1)} %copy.37) | copy-start | bytes 30724
  9.7 21.1 %copy-start.22 = (f32[1024]{0:T(1024)S(1)}, f32[1024]{0:T(1024)}, u32[]{:S(2)}) copy-start(f32[1024]{0:T(1024)} %param.15) | copy-start | bytes 12292
  61.0 4.1 copy-start.2
  61.0 4.1 copy-start.11
  61.0 4.1 copy-start.21
  70.5 2.4 copy-start.4
  72.9 1.8 copy-start.20
  72.9 2.6 copy-start.15
  74.2 320.4 %reduce-scatter.2.cloned.1.call-start = ((), (), s32[]{:S(2)}) async-start(), calls=%async_computation.2 | async-start | bytes 11796480 | tf_op jit(solution)/shard_map/reduce_scatter | solution.py:291
  112.3 13.0 %copy-start.19 = (f32[128,20]{0,1:T(8,128)S(1)}, f32[128,20]{0,1:T(8,128)}, u32[]{:S(2)}) copy-start(f32[128,20]{0,1:T(8,128)} %param.13) | copy-start | bytes 30724
  311.0 340.3 %all-gather.11.cloned.1.call-start = ((), (), s32[]{:S(2)}) async-start(), calls=%async_computation.3 | async-start | bytes 11796480 | tf_op jit(solution)/shard_map/all_gather | solution.py:304
  394.6 1.9 copy-start.3
  394.6 1.9 copy-start.12
  394.6 1.9 copy-start.14
  396.5 1.3 copy-start.7
  396.5 1.7 copy-start.8
  399.8 0.8 copy-start.5
  402.5 0.8 copy-start.10
  402.5 1.5 copy-start.13
  402.5 269.9 %all-reduce.2.cloned.1.call-start = ((), (), s32[]{:S(2)}) async-start(), calls=%async_computation.4 | async-start | bytes 8388608 | tf_op jit(solution)/shard_map/psum | solution.py:309
  508.7 1.6 copy-start.6
  606.9 2.8 copy-start.16
  606.9 2.8 copy-start.17
  607.0 2.8 copy-start.18
  672.4 4.9 copy-start.1
Sparse Core Ops, SparseCore 0:
  74.3 236.6 all-gather.8
  315.1 79.4 reduce-scatter.1
  402.7 62.9 all-gather.10
  514.9 142.1 all-reduce.1

commit v2 on v1

v2 whole, which is shorter than its diff:
```python
import functools

import jax
import jax.numpy as jnp
from jax import lax
from jax.experimental import pallas as pl
from jax.experimental.pallas import tpu as pltpu
from jax.sharding import PartitionSpec as P

LN_EPS = 1e-12
LOSS_EPS = 1e-5
VMEM_LIMIT = 60 * 1024 * 1024
ROW_CHUNK = 512
BLOCK_N = 512
DT_BLOCK = 256
GROUP = 8
WINDOW = 176
PACKED_ROWS = 1536


def gelu_norm(pre_act, gamma, beta):
    activated = jax.nn.gelu(pre_act, approximate=False)
    mean_val = jnp.mean(activated, axis=-1, keepdims=True)
    centered = activated - mean_val
    variance = jnp.mean(centered * centered, axis=-1, keepdims=True)
    return centered * lax.rsqrt(variance + LN_EPS) * gamma + beta


def over_rows(rows, unrolled, step, carry):
    full = rows // ROW_CHUNK
    if unrolled:
        for i in range(full):
            carry = step(i * ROW_CHUNK, ROW_CHUNK, carry)
    else:
        carry = lax.fori_loop(0, full, lambda i, c: step(pl.multiple_of(i * ROW_CHUNK, ROW_CHUNK), ROW_CHUNK, c), carry)
    if rows % ROW_CHUNK:
        carry = step(full * ROW_CHUNK, rows % ROW_CHUNK, carry)
    return carry


def params(**kw):
    return pltpu.CompilerParams(vmem_limit_bytes=VMEM_LIMIT, **kw)


def base_of(off_ref, g, slots):
    return pl.multiple_of(jnp.minimum(off_ref[g * GROUP] // 16, (slots - WINDOW) // 16) * 16, 16)


def pick_kernel(bounds_ref, off_ref, seat_ref, rowpos_ref, hid_ref, out_ref):
    k = pl.program_id(0)
    slots = out_ref.shape[0]
    depth, held = hid_ref.shape[0], rowpos_ref.shape[0]
    g = bounds_ref[0] + k

    @pl.when(k == 0)
    def _():
        out_ref[...] = jnp.zeros_like(out_ref)

    @pl.when(g < bounds_ref[1])
    def _():
        base = base_of(off_ref, g, slots)
        hot = (rowpos_ref[...] == lax.broadcasted_iota(jnp.int32, (held, depth), 1)).astype(jnp.bfloat16)
        move = (seat_ref[0] - base == lax.broadcasted_iota(jnp.int32, (WINDOW, held), 0)).astype(jnp.bfloat16)
        hot = jnp.dot(move, hot, preferred_element_type=jnp.float32).astype(jnp.bfloat16)
        got = jnp.dot(hot, hid_ref[...], preferred_element_type=jnp.float32)
        window = pl.ds(base, WINDOW)
        out_ref[window, :] = (out_ref[window, :].astype(jnp.float32) + got).astype(jnp.bfloat16)


def pick(hidden, rowpos_col, seat_row, bounds, offset, slots):
    groups = hidden.shape[0] // GROUP
    depth = GROUP * hidden.shape[1]
    width = hidden.shape[2]
    held = seat_row.shape[2]

    def at(k, bounds):
        return jnp.minimum(jnp.minimum(bounds[0] + k, bounds[1] - 1), groups - 1)

    return pl.pallas_call(
        pick_kernel,
        grid_spec=pltpu.PrefetchScalarGridSpec(
            num_scalar_prefetch=2,
            grid=(groups,),
            in_specs=[
                pl.BlockSpec((1, 1, held), lambda k, bounds, off: (at(k, bounds), 0, 0)),
                pl.BlockSpec((held, 1), lambda k, bounds, off: (at(k, bounds), 0)),
                pl.BlockSpec((depth, width), lambda k, bounds, off: (at(k, bounds), 0)),
            ],
            out_specs=pl.BlockSpec((slots, width), lambda k, bounds, off: (0, 0)),
        ),
        out_shape=jax.ShapeDtypeStruct((slots, width), jnp.bfloat16),
        compiler_params=params(),
        cost_estimate=pl.CostEstimate(flops=2 * WINDOW * groups * depth * width, bytes_accessed=hidden.size * 2, transcendentals=0),
        name="pick",
    )(bounds, offset, seat_row, rowpos_col, hidden.reshape(groups * depth, width))


def put_kernel(off_ref, seat_ref, rowpos_ref, dh_ref, out_ref):
    depth, held = out_ref.shape[0], seat_ref.shape[0]
    base = base_of(off_ref, pl.program_id(0), dh_ref.shape[0])
    move = (seat_ref[...] - base == lax.broadcasted_iota(jnp.int32, (held, WINDOW), 1)).astype(jnp.bfloat16)
    rows = dh_ref[pl.ds(base, WINDOW), :].astype(jnp.bfloat16)
    rows = jnp.dot(move, rows, preferred_element_type=jnp.float32).astype(jnp.bfloat16)
    hot = (rowpos_ref[0] == lax.broadcasted_iota(jnp.int32, (depth, held), 0)).astype(jnp.bfloat16)
    out_ref[...] = jnp.dot(hot, rows, preferred_element_type=jnp.float32).astype(jnp.bfloat16)


def put(d_rows, rowpos_row, seat_col, offset, batch, seq_len):
    groups = batch // GROUP
    depth = GROUP * seq_len
    slots, width = d_rows.shape
    held = rowpos_row.shape[2]
    out = pl.pallas_call(
        put_kernel,
        grid_spec=pltpu.PrefetchScalarGridSpec(
            num_scalar_prefetch=1,
            grid=(groups,),
            in_specs=[
                pl.BlockSpec((held, 1), lambda g, off: (g, 0)),
                pl.BlockSpec((1, 1, held), lambda g, off: (g, 0, 0)),
                pl.BlockSpec((slots, width), lambda g, off: (0, 0), pipeline_mode=pl.Buffered(1)),
            ],
            out_specs=pl.BlockSpec((depth, width), lambda g, off: (g, 0)),
        ),
        out_shape=jax.ShapeDtypeStruct((groups * depth, width), jnp.bfloat16),
        compiler_params=params(),
        cost_estimate=pl.CostEstimate(flops=2 * WINDOW * groups * depth * width, bytes_accessed=groups * depth * width * 2, transcendentals=0),
        name="put",
    )(offset, seat_col, rowpos_row, d_rows)
    return out.reshape(batch, seq_len, width)


def logits_kernel(unrolled, which_ref, t_ref, embed_ref, bias_ref, lab_ref, z_ref, stat_ref):
    del which_ref
    t_blk = t_ref[...].astype(jnp.bfloat16)
    lab = lab_ref[...]
    cols = t_blk.shape[0]

    def step(start, size, carry):
        top, total, target = carry
        rows = pl.ds(start, size)
        z = lax.dot_general(embed_ref[rows, :], t_blk, (((1,), (1,)), ((), ())), preferred_element_type=jnp.float32)
        z = z + bias_ref[rows, :]
        z_ref[rows, :] = z
        new_top = jnp.maximum(top, jnp.max(z, axis=0, keepdims=True))
        total = total * jnp.exp(top - new_top) + jnp.sum(jnp.exp(z - new_top), axis=0, keepdims=True)
        hot = lab - start == lax.broadcasted_iota(jnp.int32, (size, cols), 0)
        target = target + jnp.sum(jnp.where(hot, z, 0.0), axis=0, keepdims=True)
        return new_top, total, target

    zero = jnp.zeros((1, cols), jnp.float32)
    first = (jnp.full((1, cols), -jnp.inf, jnp.float32), zero, zero)
    top, total, target = over_rows(embed_ref.shape[0], unrolled, step, first)
    stat_ref[0:1, :] = top
    stat_ref[1:2, :] = total
    stat_ref[2:3, :] = target
    stat_ref[3:8, :] = jnp.zeros((5, cols), jnp.float32)


def block_map(planes, per_plane):
    if planes == 0:
        return lambda k, which: k
    return lambda k, which: lax.rem(which[0] + 1 + k // per_plane, planes) * per_plane + lax.rem(k, per_plane)


def logits_call(unrolled, which, t_rows, embed, bias_col, lab_row, planes, per_plane):
    slots = lab_row.shape[1]
    vocab, width = embed.shape
    where = block_map(planes, per_plane)
    return pl.pallas_call(
        functools.partial(logits_kernel, unrolled),
        grid_spec=pltpu.PrefetchScalarGridSpec(
            num_scalar_prefetch=1,
            grid=(slots // BLOCK_N,),
            in_specs=[
                pl.BlockSpec((BLOCK_N, width), lambda k, which: (where(k, which), 0)),
                pl.BlockSpec((vocab, width), lambda k, which: (0, 0), pipeline_mode=pl.Buffered(1)),
                pl.BlockSpec((vocab, 1), lambda k, which: (0, 0), pipeline_mode=pl.Buffered(1)),
                pl.BlockSpec((1, BLOCK_N), lambda k, which: (0, k)),
            ],
            out_specs=[
                pl.BlockSpec((vocab, BLOCK_N), lambda k, which: (0, k)),
                pl.BlockSpec((8, BLOCK_N), lambda k, which: (0, k)),
            ],
        ),
        out_shape=[jax.ShapeDtypeStruct((vocab, slots), jnp.float32), jax.ShapeDtypeStruct((8, slots), jnp.float32)],
        compiler_params=params(),
        cost_estimate=pl.CostEstimate(flops=2 * slots * vocab * width, bytes_accessed=slots * vocab * 4, transcendentals=slots * vocab),
        name="logits",
    )(which, t_rows, embed, bias_col, lab_row)


def dz_of(z, stat_ref, lab, start):
    soft = jnp.exp(z - stat_ref[0:1, :]) * stat_ref[1:2, :]
    hot = lab - start == lax.broadcasted_iota(jnp.int32, z.shape, 0)
    return jnp.where(hot, soft - 1.0, soft) * stat_ref[2:3, :]


def dt_kernel(unrolled, z_ref, stat_ref, lab_ref, embed_ref, dt_ref):
    lab = lab_ref[...]

    def step(start, size, acc):
        rows = pl.ds(start, size)
        dz = dz_of(z_ref[rows, :], stat_ref, lab, start).astype(jnp.bfloat16)
        return acc + lax.dot_general(dz, embed_ref[rows, :], (((0,), (0,)), ((), ())), preferred_element_type=jnp.float32)

    dt_ref[...] = over_rows(embed_ref.shape[0], unrolled, step, jnp.zeros(dt_ref.shape, jnp.float32))


def dt_call(unrolled, z, stat, lab_row, embed):
    slots = z.shape[1]
    vocab, width = embed.shape
    block = DT_BLOCK
    return pl.pallas_call(
        functools.partial(dt_kernel, unrolled),
        grid=(slots // block,),
        in_specs=[
            pl.BlockSpec((vocab, block), lambda k: (0, k)),
            pl.BlockSpec((8, block), lambda k: (0, k)),
            pl.BlockSpec((1, block), lambda k: (0, k)),
            pl.BlockSpec((vocab, width), lambda k: (0, 0), pipeline_mode=pl.Buffered(1)),
        ],
        out_specs=pl.BlockSpec((block, width), lambda k: (k, 0)),
        out_shape=jax.ShapeDtypeStruct((slots, width), jnp.float32),
        compiler_params=params(),
        cost_estimate=pl.CostEstimate(flops=2 * slots * vocab * width, bytes_accessed=slots * vocab * 4, transcendentals=slots * vocab),
        name="dt",
    )(z, stat, lab_row, embed)


def de_kernel(unrolled, first, part, which_ref, z_ref, stat_ref, lab_ref, t_ref, *rest):
    del which_ref
    if first:
        de_out, db_out, de_ref, db_ref, sems = rest
    else:
        de_in, db_in, de_out, db_out, de_ref, db_ref, sems = rest
    k = pl.program_id(0)
    part_rows = de_ref.shape[0]
    here = pl.ds(part * part_rows, part_rows)

    @pl.when(k == 0)
    def _():
        if first:
            de_ref[...] = jnp.zeros_like(de_ref)
            db_ref[...] = jnp.zeros_like(db_ref)
        else:
            one = pltpu.make_async_copy(de_in.at[here], de_ref, sems.at[0])
            two = pltpu.make_async_copy(db_in.at[here], db_ref, sems.at[1])
            one.start()
            two.start()
            one.wait()
            two.wait()

    lab = lab_ref[...] - part * part_rows
    t_blk = t_ref[...].astype(jnp.bfloat16)

    def step(start, size, carry):
        rows = pl.ds(start, size)
        dz = dz_of(z_ref[rows, :], stat_ref, lab, start)
        lanes = dz[:, 0:128]
        for c in range(128, dz.shape[1], 128):
            lanes = lanes + dz[:, c:c + 128]
        db_ref[rows, :] += lanes
        de_ref[rows, :] += jnp.dot(dz.astype(jnp.bfloat16), t_blk, preferred_element_type=jnp.float32)
        return carry

    over_rows(part_rows, unrolled, step, 0)

    @pl.when(k == pl.num_programs(0) - 1)
    def _():
        one = pltpu.make_async_copy(de_ref, de_out.at[here], sems.at[0])
        two = pltpu.make_async_copy(db_ref, db_out.at[here], sems.at[1])
        one.start()
        two.start()
        one.wait()
        two.wait()


def de_call(unrolled, which, z, stat, lab_row, t_rows, planes, per_plane, carry=None, part=0, parts=1):
    vocab, slots = z.shape
    width = t_rows.shape[1]
    where = block_map(planes, per_plane)
    first = carry is None
    part_rows = vocab // parts
    in_specs = [
        pl.BlockSpec((part_rows, BLOCK_N), lambda k, which: (part, k)),
        pl.BlockSpec((8, BLOCK_N), lambda k, which: (0, k)),
        pl.BlockSpec((1, BLOCK_N), lambda k, which: (0, k)),
        pl.BlockSpec((BLOCK_N, width), lambda k, which: (where(k, which), 0)),
    ]
    args = [which, z, stat, lab_row, t_rows]
    aliases = {}
    if not first:
        in_specs += [pl.BlockSpec(memory_space=pl.ANY), pl.BlockSpec(memory_space=pl.ANY)]
        args += list(carry)
        aliases = {5: 0, 6: 1}
    return pl.pallas_call(
        functools.partial(de_kernel, unrolled, first, part),
        grid_spec=pltpu.PrefetchScalarGridSpec(
            num_scalar_prefetch=1,
            grid=(slots // BLOCK_N,),
            in_specs=in_specs,
            out_specs=[pl.BlockSpec(memory_space=pl.ANY), pl.BlockSpec(memory_space=pl.ANY)],
            scratch_shapes=[pltpu.VMEM((part_rows, width), jnp.float32), pltpu.VMEM((part_rows, 128), jnp.float32), pltpu.SemaphoreType.DMA((2,))],
        ),
        out_shape=[jax.ShapeDtypeStruct((vocab, width), jnp.float32), jax.ShapeDtypeStruct((vocab, 128), jnp.float32)],
        input_output_aliases=aliases,
        compiler_params=params(),
        cost_estimate=pl.CostEstimate(flops=2 * slots * part_rows * width, bytes_accessed=slots * part_rows * 4, transcendentals=slots * part_rows),
        name="de",
    )(*args)


def combine(stat, weights_row, denom):
    parts = lax.all_gather(stat[:3], "tp", axis=0)
    top = jnp.max(parts[:, 0], axis=0)
    total = jnp.sum(parts[:, 1] * jnp.exp(parts[:, 0] - top[None]), axis=0)
    target = jnp.sum(parts[:, 2], axis=0)
    zero = jnp.zeros_like(top)
    rows = jnp.stack([top, 1.0 / total, weights_row / denom, zero, zero, zero, zero, zero])
    return rows, jnp.log(total) + top - target


def packed(values, index, slots):
    hot = index[..., None, :] == jnp.arange(slots, dtype=jnp.int32)[:, None]
    return jnp.sum(jnp.where(hot, values[..., None, :], 0), axis=-1)


def solution(mesh):
    dp, tp = mesh.shape["dp"], mesh.shape["tp"]

    def body(unrolled, slots, hidden, positions, weights, small, counts, w_t, b_t, gamma, beta, embed, out_bias):
        batch, seq_len, width = hidden.shape
        max_pred = positions.shape[1]
        shard_vocab = embed.shape[0]
        groups = batch // GROUP
        share = slots // tp
        per_plane = slots // BLOCK_N
        dp_idx, tp_idx = lax.axis_index("dp"), lax.axis_index("tp")
        which = dp_idx.reshape(1).astype(jnp.int32)
        denom = jnp.sum(counts).astype(jnp.float32) + LOSS_EPS

        column = jnp.arange(max_pred, dtype=jnp.int32)
        before = (jnp.arange(batch)[:, None] > jnp.arange(batch)[None, :]).astype(jnp.float32)
        by_seq = jnp.sum(weights, axis=1)
        offset = jnp.sum(before * by_seq[None, :], axis=1).astype(jnp.int32)
        seat = jnp.where(weights > 0, offset[:, None] + column, -WINDOW * batch)
        first_of = offset.reshape(groups, GROUP)[:, 0]
        ends = first_of + jnp.sum(by_seq.reshape(groups, GROUP), axis=1).astype(jnp.int32)
        row_of = positions + (jnp.arange(batch, dtype=jnp.int32) % GROUP * seq_len)[:, None]
        rowpos_col = row_of.reshape(-1, 1)
        seat_row = seat.reshape(groups, 1, -1)

        def transform(rows):
            pre_act = jnp.dot(rows, w_t, preferred_element_type=jnp.float32) + b_t
            return gelu_norm(pre_act, gamma, beta).astype(jnp.bfloat16)

        low = tp_idx * share
        bounds = jnp.sum(jnp.stack([ends <= low, first_of < low + share]).astype(jnp.int32), axis=1)
        some = pick(hidden, rowpos_col, seat_row, bounds, offset, slots)
        part_rows = lax.dynamic_slice_in_dim(some, low, share, 0)
        t_part = lax.optimization_barrier(transform(part_rows).astype(jnp.float32))
        t_all = lax.all_gather(t_part, ("dp", "tp"), axis=0, tiled=True)

        small, held, bias_col, t_part = lax.optimization_barrier((small, hidden, out_bias, t_part))
        bias_col = bias_col.reshape(-1, 1)
        every = jnp.array([0, groups], jnp.int32)
        tok_rows = pick(held, rowpos_col, seat_row, every, offset, slots)
        pre_act = jnp.dot(tok_rows, w_t, preferred_element_type=jnp.float32) + b_t
        normed, norm_vjp = jax.vjp(gelu_norm, pre_act, gamma, beta)
        t_own = normed.astype(jnp.bfloat16)

        turned = lax.dynamic_slice_in_dim(jnp.concatenate([small, small]), dp_idx, dp, 0)
        ahead = jnp.sum(jnp.where(before[None] > 0, jnp.sum(turned[:, 1].reshape(dp, 1, batch, max_pred), axis=3), 0.0), axis=2)
        index = jnp.where(turned[:, 1].reshape(dp, batch, max_pred) > 0, ahead[:, :, None].astype(jnp.int32) + column, -1)
        index = index.reshape(dp, batch * max_pred)
        labels = turned[:, 0].astype(jnp.int32) - tp_idx * shard_vocab
        total = jnp.sum(turned[:, 1], axis=1)
        weight_rows = (jnp.arange(slots, dtype=jnp.int32)[None, :] < total[:, None].astype(jnp.int32)).astype(jnp.float32)
        own_lab = packed(labels[:1], index[:1], slots)
        z_own, stat_own = logits_call(unrolled, which, t_own, embed, bias_col, own_lab, 0, per_plane)
        rows_own, ce = combine(stat_own, weight_rows[0], denom)
        dt_part = dt_call(unrolled, z_own, rows_own, own_lab, embed)
        d_normed = lax.psum(dt_part, "tp")
        carry = de_call(unrolled, which, z_own, rows_own, own_lab, t_own, 0, per_plane)
        far_lab = packed(labels[1:], index[1:], slots).reshape(1, -1)
        loss = jnp.sum(weight_rows[0] * ce)

        t_all, carry, far_lab = lax.optimization_barrier((t_all, carry, far_lab))
        z_far, stat_far = logits_call(unrolled, which, t_all, embed, bias_col, far_lab, dp, per_plane)
        rows_far, _ = combine(stat_far, weight_rows[1:].reshape(-1), denom)

        d_normed, rows_far = lax.optimization_barrier((d_normed, rows_far))
        d_pre, d_gamma, d_beta = norm_vjp(d_normed)
        d_pre_bf = d_pre.astype(jnp.bfloat16)
        d_rows = jnp.einsum("ne,de->nd", d_pre_bf, w_t, preferred_element_type=jnp.float32).astype(jnp.bfloat16)
        cut = width // tp
        part_cols = lax.dynamic_slice_in_dim(tok_rows, tp_idx * cut, cut, 1)
        d_w_t = jnp.einsum("nd,ne->de", part_cols, d_pre_bf, preferred_element_type=jnp.float32)
        vecs = [jnp.sum(d_pre, axis=0)[None], d_gamma[None], d_beta[None], jnp.full((5, width), loss)]
        block = jnp.concatenate([d_w_t] + vecs)
        d_rows, block, de_sum, db_sum = lax.optimization_barrier((d_rows, block, *carry))
        block = lax.psum(block, "dp")
        carry = de_call(unrolled, which, z_far, rows_far, far_lab, t_all, dp, per_plane, (de_sum, db_sum), 0, 2)
        block, de_sum, db_sum = lax.optimization_barrier((block, *carry))
        d_w_t = lax.all_gather(block[:cut], "tp", axis=0, tiled=True)
        d_embed, d_bias = de_call(unrolled, which, z_far, rows_far, far_lab, t_all, dp, per_plane, (de_sum, db_sum), 1, 2)
        d_rows, d_bias = lax.optimization_barrier((d_rows, d_bias))
        d_hidden = put(d_rows, row_of.reshape(groups, 1, -1), seat.reshape(-1, 1), offset, batch, seq_len)
        d_out_bias = jnp.sum(d_bias, axis=1)
        return block[cut + 3, 0] / denom, d_hidden, d_w_t, block[cut], block[cut + 1], block[cut + 2], d_embed, d_out_bias

    def local_step(hidden, positions, labels, weights, w_t, b_t, gamma, beta, embed, out_bias):
        small = jnp.stack([labels.reshape(-1).astype(jnp.float32), weights.reshape(-1)])
        small = lax.all_gather(small, "dp", axis=0)
        counts = jnp.sum((small[:, 1] > 0).astype(jnp.int32), axis=1)
        fits = jnp.max(counts) <= PACKED_ROWS
        args = (hidden, positions, weights, small, counts, w_t, b_t, gamma, beta, embed, out_bias)
        return lax.cond(fits, functools.partial(body, True, PACKED_ROWS), functools.partial(body, False, labels.size), *args)

    in_specs = (P("dp", None, None), P("dp", None), P("dp", None), P("dp", None), P(None, None), P(None), P(None), P(None), P("tp", None), P("tp"))
    out_specs = (P(), P("dp", None, None), P(None, None), P(None), P(None), P(None), P("tp", None), P("tp"))
    return jax.shard_map(local_step, mesh=mesh, in_specs=in_specs, out_specs=out_specs, check_vma=False)
```

time: 693 us -> 469 us (0.68)
  waiting for transfers between devices: 179 us -> 48.7 us
  Pallas kernels: 326 us -> 253 us
  blocking collectives: 75.9 us -> 38.1 us
  other arithmetic: 20.3 us -> 39.7 us
  matrix products: 42.5 us -> 30 us
  loops' own time: 0 us -> 7.82 us
    all_gather x2, waiting for transfers between devices: 103 us -> 10.2 us  [the longest x1 10.2 us: body(): t_all = lax.all_gather(t_part, ('dp', 'tp'), axis=0, tiled=True)]
    reduce_scatter x1 -> x0, waiting for transfers between devices: 76.8 us -> none  [local_step(): d_normed = lax.psum_scatter(dt_part, 'tp', scatter_dimension=0, tiled=True)]
    pallas_call x7 -> x9, Pallas kernels: 326 us -> 253 us  [the longest x3 95.5 us: de_call(): pl.pallas_call(functools.partial(de_kernel, unrolled, first, part), grid_...]
    psum x1 -> x0, blocking collectives: 39.7 us -> none  [local_step(): d_w_t, vecs = lax.psum((d_w_t, vecs), ('dp', 'tp'))]
    psum x1 -> x2, waiting for transfers between devices: 0.01 us -> 38.4 us  [the longest x1 34.3 us: body(): d_normed = lax.psum(dt_part, 'tp')]
    reduce_sum x5 -> x14, other arithmetic: 6.81 us -> 19.9 us  [the longest x2 7.58 us: packed(): return jnp.sum(jnp.where(hot, values[..., None, :], 0), axis=-1)]
    dot_general x4, matrix products: 42.5 us -> 30 us  [the longest x1 20 us: body(): pre_act = jnp.dot(tok_rows, w_t, preferred_element_type=jnp.float32) + b_t]
    reduce_sum x1 -> x2, other arithmetic: 1.85 us -> 11.9 us  [gelu_norm(): return centered * lax.rsqrt(variance + LN_EPS) * gamma + beta]
  transfers between devices with their start and end apart: 4 -> 4, of which waited for: 2 -> 3; matrix products, arithmetic and copies ran while one was open for 4% -> 10% of each run, Pallas kernels for 45% -> 53%
where the time goes in v2:
time: 469 us; the launch traced here: 460 us
  Pallas kernels  253 us (54%)
  waiting for transfers between devices  48.7 us (10%)
  other arithmetic  39.7 us (8%)
  blocking collectives  38.1 us (8%)
  matrix products  30 us (6%)
  local copies, waits for them, and re-layouts  26.1 us (6%)
  between operations  16.1 us (3%)
  loops' own time  7.82 us (2%)
    pallas_call x3, Pallas kernels, de_call(): pl.pallas_call(functools.partial(de_kernel, unrolled, first, part), grid_...  95.5 us
    pallas_call x2, Pallas kernels, logits_call(): pl.pallas_call(functools.partial(logits_kernel, unrolled), grid_spec=pltp...  82.4 us
    psum x1, waiting for transfers between devices, body(): d_normed = lax.psum(dt_part, 'tp')  34.3 us
    pallas_call x2, Pallas kernels, pick(): pl.pallas_call(pick_kernel, grid_spec=pltpu.PrefetchScalarGridSpec(num_sc...  31.9 us
    all_gather x2, blocking collectives, combine(): parts = lax.all_gather(stat[:3], 'tp', axis=0)  23.2 us
    pallas_call x1, Pallas kernels, put(): pl.pallas_call(put_kernel, grid_spec=pltpu.PrefetchScalarGridSpec(num_sca...  21.6 us
    pallas_call x1, Pallas kernels, dt_call(): pl.pallas_call(functools.partial(dt_kernel, unrolled), grid=(slots // blo...  21.4 us
    dot_general x1, matrix products, body(): pre_act = jnp.dot(tok_rows, w_t, preferred_element_type=jnp.float32) + b_t  20 us
  transfers between devices with their start and end apart: 4, of which 3 were waited for; matrix products, arithmetic and copies ran while one was open for 10% of the time, Pallas kernels for 53%

profile of v2, /device:TPU:0, one launch (start us, length us, event | category | flops | bytes accessed | tf_op | source)
XLA Modules:
  0.0 459.8 jit_solution(8923720081195351352)
XLA Ops:
  7.2 0.7 convert_element_type.158
  8.1 0.8 copy.155
  9.1 14.9 %all-gather.9 = f32[4,2,2560]{2,1,0:T(2,128)S(1)} all-gather(f32[1,2,2560]{2,1,0:T(2,128)S(1)} %maximum_bitcast_fusion), channel_id=6, replica_groups=mesh['dp'=4,'tp'=8] {'dp'}, dimensions={0}, use_global_device_ids=true | all-gather | bytes 102400 | tf_op jit(solution)/shard_map/all_gather | solution.py:415
  24.0 0.2 fusion.78
  24.2 0.6 reduce_max.45
  25.5 421.3 %conditional.1 = (f32[3824,1024]{1,0:T(8,128)}, f32[]{:T(128)}, bf16[128,128,1024]{2,1,0:T(8,128)(2,1)}, f32[1024,1024]{1,0:T(8,128)}, f32[1024]{0:T(1024)S(1)},...) conditional(s32[]{:T(128)} %convert_element_type.161, (f32[128,20]{0,1:T(8,128)}, ...), branch_computations={%region_2.31_spmd, %region_31.60_spmd} | conditional | flops 210638716928 | bytes 988409216 | solution.py:419
  31.1 0.7 reduce_sum.419
  32.1 0.8 copy.159
  33.2 0.8 copy.160
  34.2 0.7 reshape.600.seat_ref
  35.0 1.5 reshape.601.rowpos_ref
  36.4 0.6 fusion.73.bounds_ref
  37.1 8.1 %pick.6 = bf16[1536,1024]{1,0:T(8,128)(2,1)} custom-call(s32[2]{0:T(128)} %fusion.73.bounds_ref, s32[128]{0:T(128)} %copy-done.25, s32[16,1,160]{2,1,0:T(1,128)} %reshape.600.seat_ref, s32[2560,1]{1,0:T(8,128)} %reshape.601.rowpos_ref, bf16[16384,1024]{1,0:T(8,128)(2,1)} %bitcast.130), custom_call_target="tpu_custom_call" | custom-call | flops 5905580032 | bytes 33554432 | tf_op jit(solution)/shard_map/cond/branch_1_fun/pick/pallas_call | solution.py:79
  45.3 3.3 fusion.94
  48.6 0.2 multiply_reduce_fusion.8
  48.9 1.1 fusion.58
  50.0 0.6 reduce_sum.465
  51.6 0.3 squeeze.52
  52.6 1.7 select_reduce_fusion.5
  54.3 0.6 reduce_sum.462.lab_ref
  54.9 1.8 reshape.602.bias_ref
  56.8 0.5 broadcast_multiply_fusion.5.bounds_ref
  57.3 23.7 %pick.7 = bf16[1536,1024]{1,0:T(8,128)(2,1)} custom-call(s32[2]{0:T(128)} %broadcast_multiply_fusion.5.bounds_ref, s32[128]{0:T(128)} %copy-done.25, s32[16,1,160]{2,1,0:T(1,128)} %reshape.600.seat_ref, s32[2560,1]{1,0:T(8,128)} %reshape.601.rowpos_ref, bf16[16384,1024]{1,0:T(8,128)(2,1)} %bitcast.131), custom_call_target="tpu_custom_call" | custom-call | flops 5905580032 | bytes 33554432 | tf_op jit(solution)/shard_map/cond/branch_1_fun/pick/pallas_call | solution.py:79
  81.0 20.0 %fusion.85 = (f32[1536]{0:T(1024)S(1)}, f32[1536,1024]{1,0:T(8,128)S(1)}, f32[1536,1024]{1,0:T(8,128)}, f32[1536,1024]{1,0:T(8,128)}) fusion(f32[1024]{0:T(1024)S(1)} %copy-done.24, bf16[1536,1024]{1,0:T(8,128)(2,1)} %pick.7, bf16[1024,1024]{1,0:T(8,128)(2,1)S(1)} %copy-done.32), kind=kOutput, calls=%fused_computation.232 | convolution fusion | flops 3325032960 | bytes 24127488 | tf_op jit(solution)/shard_map/cond/branch_1_fun/dot_general | solution.py:369
  101.0 0.8 multiply_reduce_fusion.7
  101.8 2.8 add_convert_fusion.3.t_ref
  104.6 24.1 %logits.6 = (f32[3824,1536]{1,0:T(8,128)}, f32[8,1536]{1,0:T(8,128)}) custom-call(s32[1]{0:T(128)} %bitcast.17.which_ref, bf16[1536,1024]{1,0:T(8,128)(2,1)} %add_convert_fusion.3.t_ref, bf16[3824,1024]{1,0:T(8,128)(2,1)} %get-tuple-element.178.embed_ref, f32[3824,1]{1,0:T(8,128)} %reshape.602.bias_ref, s32[1,1536]{1,0:T(1,128)} %reduce_sum.462.lab_ref), custom_call_target="tpu_custom_call" | custom-call | flops 12029263872 | bytes 23494656 | tf_op jit(solution)/shard_map/cond/branch_1_fun/logits/pallas_call | solution.py:170
  128.7 0.8 slice_bitcast_fusion.5
  129.5 10.1 %all-gather.7 = f32[8,3,1536]{2,1,0:T(4,128)S(1)} all-gather(f32[1,3,1536]{2,1,0:T(4,128)S(1)} %slice_bitcast_fusion.5), channel_id=4, replica_groups=mesh['dp'=4,'tp'=8] {'tp'}, dimensions={0}, use_global_device_ids=true | all-gather | bytes 165888 | tf_op jit(solution)/shard_map/cond/branch_1_fun/all_gather | solution.py:315
  139.6 0.1 fusion.93
  139.9 0.6 multiply_reduce_fusion.9
  140.6 0.7 stack.29.stat_ref
  141.2 21.4 %dt.3 = f32[1536,1024]{1,0:T(8,128)} custom-call(f32[3824,1536]{1,0:T(8,128)} %get-tuple-element.102.z_ref, f32[8,1536]{1,0:T(8,128)} %stack.29.stat_ref, s32[1,1536]{1,0:T(1,128)} %reduce_sum.462.lab_ref, bf16[3824,1024]{1,0:T(8,128)(2,1)} %get-tuple-element.178.embed_ref), custom_call_target="tpu_custom_call" | custom-call | flops 12029263872 | bytes 23494656 | tf_op jit(solution)/shard_map/cond/branch_1_fun/dt/pallas_call | solution.py:214
  162.8 26.0 %de.9 = (f32[3824,1024]{1,0:T(8,128)}, f32[3824,128]{1,0:T(8,128)}) custom-call(s32[1]{0:T(128)} %bitcast.17.which_ref, f32[3824,1536]{1,0:T(8,128)} %get-tuple-element.102.z_ref, f32[8,1536]{1,0:T(8,128)} %stack.29.stat_ref, s32[1,1536]{1,0:T(1,128)} %reduce_sum.462.lab_ref, bf16[1536,1024]{1,0:T(8,128)(2,1)} %add_convert_fusion.3.t_ref), custom_call_target="tpu_custom_call" | custom-call | flops 12029263872 | bytes 23494656 | tf_op jit(solution)/shard_map/cond/branch_1_fun/de/pallas_call | solution.py:297
  188.8 0.2 eq.75
  189.0 5.8 %select_reduce_fusion.4 = s32[3,1536]{1,0:T(4,128)S(1)} fusion(s32[3,2560]{1,0:T(4,128)S(1)} %slice_bitcast_fusion.4, s32[3,2560]{1,0:T(4,128)S(1)} %eq.75), kind=kLoop, calls=%fused_computation.112 | loop fusion | flops 35384832 | bytes 79872 | tf_op jit(solution)/shard_map/cond/branch_1_fun/reduce_sum | solution.py:326
  194.8 0.6 copy.178
  195.4 10.2 %all-gather.19.cloned.1.call-done.t_ref = f32[6144,1024]{1,0:T(8,128)} async-done(((f32[192,1024]{1,0:T(8,128)}), f32[6144,1024]{1,0:T(8,128)}) %all-gather.19.cloned.1.call-update) | async-done | bytes 25165840 | tf_op jit(solution)/shard_map/cond/branch_1_fun/all_gather | solution.py:363
  205.6 58.3 %logits.7 = (f32[3824,4608]{1,0:T(8,128)}, f32[8,4608]{1,0:T(8,128)}) custom-call(s32[1]{0:T(128)} %bitcast.17.which_ref, f32[6144,1024]{1,0:T(8,128)} %all-gather.19.cloned.1.call-done.t_ref, bf16[3824,1024]{1,0:T(8,128)(2,1)} %get-tuple-element.178.embed_ref, f32[3824,1]{1,0:T(8,128)} %reshape.602.bias_ref, s32[1,4608]{1,0:T(1,128)} %bitcast.143), custom_call_target="tpu_custom_call" | custom-call | flops 36087791616 | bytes 70483968 | tf_op jit(solution)/shard_map/cond/branch_1_fun/logits/pallas_call | solution.py:170
  263.9 0.9 slice_bitcast_fusion.3
  264.8 13.1 %all-gather.8 = f32[8,3,4608]{2,1,0:T(4,128)S(1)} all-gather(f32[1,3,4608]{2,1,0:T(4,128)S(1)} %slice_bitcast_fusion.3), channel_id=5, replica_groups=mesh['dp'=4,'tp'=8] {'tp'}, dimensions={0}, use_global_device_ids=true | all-gather | bytes 497664 | tf_op jit(solution)/shard_map/cond/branch_1_fun/all_gather | solution.py:315
  277.9 0.3 fusion.91
  278.4 0.8 stack.31.stat_ref
  279.2 34.3 %all-reduce.9.cloned.1.call-done = f32[1536,1024]{1,0:T(8,128)} async-done(((f32[1536,1024]{1,0:T(8,128)}), f32[1536,1024]{1,0:T(8,128)}) %all-reduce.9.cloned.1.call-update) | async-done | bytes 6291472 | tf_op jit(solution)/shard_map/cond/branch_1_fun/psum | solution.py:384
  313.5 5.7 %fusion.80 = (f32[1024]{0:T(1024)S(1)}, f32[1536]{0:T(1024)S(1)}) fusion(f32[1536,1024]{1,0:T(8,128)} %all-reduce.9.cloned.1.call-done, f32[1024]{0:T(1024)S(1)} %copy-done.15, f32[1536,1024]{1,0:T(8,128)} %copy-done.1, f32[1536]{0:T(1024)S(1)} %broadcast_multiply_fusion.3), kind=kLoop, calls=%fused_computation.228 | loop fusion | flops 7861760 | bytes 12603392 | tf_op jit(solution)/shard_map/cond/branch_1_fun/transpose(jvp())/reduce_sum | solution.py:26
  319.2 0.7 copy-done.3
  319.9 6.2 %multiply_reduce_fusion.5 = (f32[1024]{0:T(1024)S(1)}, f32[1536]{0:T(1024)S(1)}) fusion(f32[1536,1024]{1,0:T(8,128)S(1)} %copy-done.3, f32[1536,1024]{1,0:T(8,128)} %copy-done.1, f32[1536]{0:T(1024)S(1)} %fusion.72, f32[1536]{0:T(1024)S(1)} %broadcast_multiply_fusion.3, f32[1536]{0:T(1024)S(1)} %multiply_multiply_fusion.23, f32[1024]{0:T(1024)S(1)} %copy-done.15), kind=kLoop, calls=%fused_computation.119 | loop fusion | flops 15726080 | bytes 12615680 | tf_op jit(solution)/shard_map/cond/branch_1_fun/transpose(jvp())/reduce_sum | solution.py:26
  326.2 6.7 %fusion.84 = (f32[1024]{0:T(1024)S(1)}, bf16[1536,1024]{1,0:T(8,128)(2,1)S(1)}) fusion(f32[1536,1024]{1,0:T(8,128)S(1)} %bitcast.139, f32[1536]{0:T(1024)S(1)} %negate_multiply_fusion.5, f32[1536]{0:T(1024)S(1)} %multiply_multiply_fusion.23, f32[1536,1024]{1,0:T(8,128)S(1)} %bitcast.135, f32[1536]{0:T(1024)S(1)} %broadcast_multiply_fusion.3, ...), kind=kLoop, calls=%fused_computation.231 | loop fusion | flops 36174848 | bytes 28348416 | tf_op jit(solution)/shard_map/cond/branch_1_fun/reduce_sum | solution.py:400
  332.9 5.1 %convolution_convert_fusion.1.dh_ref = bf16[1536,1024]{1,0:T(8,128)(2,1)} fusion(bf16[1024,1024]{1,0:T(8,128)(2,1)S(1)} %copy-done.32, bf16[1536,1024]{1,0:T(8,128)(2,1)S(1)} %get-tuple-element.307), kind=kOutput, calls=%fused_computation.138 | convolution fusion | flops 3222798336 | bytes 8388608 | tf_op jit(solution)/shard_map/cond/branch_1_fun/ne,de->nd/dot_general | solution.py:396
  338.0 1.6 fusion.46
  339.6 0.7 broadcast_in_dim.149
  340.3 1.5 concatenate.11
  341.8 0.3 all-gather.21.cloned.1.call-start
  342.1 34.8 %de.10 = (f32[3824,1024]{1,0:T(8,128)}, f32[3824,128]{1,0:T(8,128)}) custom-call(s32[1]{0:T(128)} %bitcast.17.which_ref, f32[3824,4608]{1,0:T(8,128)} %get-tuple-element.114.z_ref, f32[8,4608]{1,0:T(8,128)} %stack.31.stat_ref, s32[1,4608]{1,0:T(1,128)} %bitcast.144, ...), custom_call_target="tpu_custom_call", output_to_operand_aliasing={{0}: (5, {}), {1}: (6, {})} | custom-call | flops 18043895808 | bytes 35241984 | tf_op jit(solution)/shard_map/cond/branch_1_fun/de/pallas_call | solution.py:297
  376.9 4.2 all-reduce.11.cloned.1.call-done
  381.1 1.9 slice.146
  383.0 0.7 reshape.596.rowpos_ref
  383.7 1.5 reshape.595.seat_ref
  385.2 1.2 slice.145
  387.0 34.8 %de.11 = (f32[3824,1024]{1,0:T(8,128)}, f32[3824,128]{1,0:T(8,128)}) custom-call(s32[1]{0:T(128)} %bitcast.17.which_ref, f32[3824,4608]{1,0:T(8,128)} %get-tuple-element.114.z_ref, f32[8,4608]{1,0:T(8,128)} %stack.31.stat_ref, s32[1,4608]{1,0:T(1,128)} %bitcast.145, ...), custom_call_target="tpu_custom_call", output_to_operand_aliasing={{0}: (5, {}), {1}: (6, {})} | custom-call | flops 18043895808 | bytes 35241984 | tf_op jit(solution)/shard_map/cond/branch_1_fun/de/pallas_call | solution.py:297
  421.8 2.1 reduce_sum.475
  423.9 0.9 fusion.92
  424.8 21.6 %put.3 = bf16[16384,1024]{1,0:T(8,128)(2,1)} custom-call(s32[128]{0:T(128)} %copy-done.25, s32[2560,1]{1,0:T(8,128)} %reshape.595.seat_ref, s32[16,1,160]{2,1,0:T(1,128)} %reshape.596.rowpos_ref, bf16[1536,1024]{1,0:T(8,128)(2,1)} %convolution_convert_fusion.1.dh_ref), custom_call_target="tpu_custom_call" | custom-call | flops 5905580032 | bytes 33554432 | tf_op jit(solution)/shard_map/cond/branch_1_fun/put/pallas_call | solution.py:113
  446.8 4.8 %copy.241 = f32[1024,1024]{1,0:T(8,128)} copy(f32[1024,1024]{1,0:T(8,128)} %get-tuple-element.383) | data formatting | bytes 8388608
  (107 shorter events, 2.5 us)
Async XLA Ops:
  31.1 6.0 %copy-start.33 = (s32[2]{0:T(128)}, s32[2]{0:T(128)S(1)}, u32[]{:S(2)}) copy-start(s32[2]{0:T(128)S(1)} %get-tuple-element.181) | copy-start | bytes 28 | tf_op jit(solution)/shard_map/cond
  31.1 174.5 %all-gather.19.cloned.1.call-start = ((), (), s32[]{:S(2)}) async-start(), calls=%async_computation.5 | async-start | bytes 25952256 | tf_op jit(solution)/shard_map/cond/branch_1_fun/all_gather | solution.py:363
  32.9 4.2 copy-start.25
  34.1 11.1 %copy-start.8 = (s32[128,20]{1,0:T(8,128)}, s32[128,20]{1,0:T(8,128)S(1)}, u32[]{:S(2)}) copy-start(s32[128,20]{1,0:T(8,128)S(1)} %add_select_fusion.3) | copy-start | bytes 30724 | tf_op jit(solution)/shard_map/cond
  35.0 10.3 %copy-start.12 = (s32[128,20]{1,0:T(8,128)}, s32[128,20]{1,0:T(8,128)S(1)}, u32[]{:S(2)}) copy-start(s32[128,20]{1,0:T(8,128)S(1)} %broadcast_add_fusion.1) | copy-start | bytes 30724 | tf_op jit(solution)/shard_map/cond
  37.1 8.1 %copy-start.24 = (f32[1024]{0:T(1024)S(1)}, f32[1024]{0:T(1024)}, u32[]{:S(2)}) copy-start(f32[1024]{0:T(1024)} %get-tuple-element.168) | copy-start | bytes 12292 | tf_op jit(solution)/shard_map/cond
  37.1 8.1 %copy-start.32 = (bf16[1024,1024]{1,0:T(8,128)(2,1)S(1)}, bf16[1024,1024]{1,0:T(8,128)(2,1)}, u32[]{:S(2)}) copy-start(bf16[1024,1024]{1,0:T(8,128)(2,1)} %get-tuple-element.166) | copy-start | bytes 6291460 | tf_op jit(solution)/shard_map/cond
  45.2 3.6 copy-start.15
  45.2 3.6 copy-start.21
  45.2 9.7 %copy-start.19 = (f32[3824]{0:T(1024)S(1)}, f32[3824]{0:T(1024)}, u32[]{:S(2)}) copy-start(f32[3824]{0:T(1024)} %get-tuple-element.100) | copy-start | bytes 45892 | tf_op jit(solution)/shard_map/cond
  48.6 8.2 %copy-start.34 = (s32[2]{0:T(128)S(1)}, s32[2]{0:T(128)}, u32[]{:S(2)}) copy-start(s32[2]{0:T(128)} %copy-done.33) | copy-start | bytes 28 | tf_op jit(solution)/shard_map/cond
  50.0 263.5 %all-reduce.9.cloned.1.call-start = ((), (), s32[]{:S(2)}) async-start(), calls=%async_computation.4 | async-start | bytes 12582912 | tf_op jit(solution)/shard_map/cond/branch_1_fun/psum | solution.py:384
  52.4 110.4 %copy-start.5 = (s32[4,128,20]{2,1,0:T(8,128)}, s32[4,128,20]{2,1,0:T(8,128)S(1)}, u32[]{:S(2)}) copy-start(s32[4,128,20]{2,1,0:T(8,128)S(1)} %add_select_fusion.2) | copy-start | bytes 122884 | tf_op jit(solution)/shard_map/cond
  101.0 3.6 copy-start.1
  162.7 218.4 %all-reduce.11.cloned.1.call-start = ((), (), s32[]{:S(2)}) async-start(), calls=%async_computation.6 | async-start | bytes 1114112 | tf_op jit(solution)/shard_map/cond/branch_1_fun/psum | solution.py:403
  162.8 26.0 %slice-start.8 = ((s32[4,128,20]{2,1,0:T(8,128)}), s32[3,128,20]{2,1,0:T(8,128)S(1)}, s32[]{:S(2)}) async-start(s32[4,128,20]{2,1,0:T(8,128)} %copy-done.5), calls=%async_computation.16 | async-start | bytes 393216 | tf_op jit(solution)/shard_map/cond/branch_1_fun/slice | solution.py:386
  313.5 6.4 %copy-start.3 = (f32[1536,1024]{1,0:T(8,128)S(1)}, f32[1536,1024]{1,0:T(8,128)}, u32[]{:S(2)}) copy-start(f32[1536,1024]{1,0:T(8,128)} %all-reduce.9.cloned.1.call-done) | copy-start | bytes 18874372 | tf_op jit(solution)/shard_map/cond
  313.5 12.6 %slice-start.3 = ((s8[6291456]{0:T(1024)(128)(4,1)}), s8[4194304]{0:T(1024)(128)(4,1)S(1)}, s32[]{:S(2)}) async-start(s8[6291456]{0:T(1024)(128)(4,1)} %bitcast.134), calls=%async_computation.11 | async-start | bytes 8388608 | tf_op jit(solution)/shard_map/cond
  313.5 12.7 %slice-start.5 = ((s8[6291456]{0:T(1024)(128)(4,1)}), s8[4194304]{0:T(1024)(128)(4,1)S(1)}, s32[]{:S(2)}) async-start(s8[6291456]{0:T(1024)(128)(4,1)} %bitcast.138), calls=%async_computation.13 | async-start | bytes 8388608 | tf_op jit(solution)/shard_map/cond
  319.9 6.2 %slice-start.4 = ((s8[6291456]{0:T(1024)(128)(4,1)}), s8[2097152]{0:T(1024)(128)(4,1)S(1)}, s32[]{:S(2)}) async-start(s8[6291456]{0:T(1024)(128)(4,1)} %bitcast.134), calls=%async_computation.12 | async-start | bytes 4194304 | tf_op jit(solution)/shard_map/cond
  319.9 6.2 %slice-start.6 = ((s8[6291456]{0:T(1024)(128)(4,1)}), s8[2097152]{0:T(1024)(128)(4,1)S(1)}, s32[]{:S(2)}) async-start(s8[6291456]{0:T(1024)(128)(4,1)} %bitcast.138), calls=%async_computation.14 | async-start | bytes 4194304 | tf_op jit(solution)/shard_map/cond
  341.8 104.7 %all-gather.21.cloned.1.call-start = ((), (), s32[]{:S(2)}) async-start(), calls=%async_computation.7 | async-start | bytes 4718592 | tf_op jit(solution)/shard_map/cond/branch_1_fun/all_gather | solution.py:406
  342.1 40.9 %copy-start.13 = (s32[128,20]{1,0:T(8,128)S(1)}, s32[128,20]{1,0:T(8,128)}, u32[]{:S(2)}) copy-start(s32[128,20]{1,0:T(8,128)} %copy-done.12) | copy-start | bytes 30724 | tf_op jit(solution)/shard_map/cond
  342.1 41.6 %copy-start.9 = (s32[128,20]{1,0:T(8,128)S(1)}, s32[128,20]{1,0:T(8,128)}, u32[]{:S(2)}) copy-start(s32[128,20]{1,0:T(8,128)} %copy-done.8) | copy-start | bytes 30724 | tf_op jit(solution)/shard_map/cond
  446.8 4.8 %copy-start.22 = (f32[3824]{0:T(1024)}, f32[3824]{0:T(1024)S(1)}, u32[]{:S(2)}) copy-start(f32[3824]{0:T(1024)S(1)} %get-tuple-element.388) | copy-start | bytes 45892
  446.8 4.8 %copy-start.27 = (f32[1024]{0:T(1024)}, f32[1024]{0:T(1024)S(1)}, u32[]{:S(2)}) copy-start(f32[1024]{0:T(1024)S(1)} %get-tuple-element.386) | copy-start | bytes 12292
  446.8 4.8 %copy-start.28 = (f32[1024]{0:T(1024)}, f32[1024]{0:T(1024)S(1)}, u32[]{:S(2)}) copy-start(f32[1024]{0:T(1024)S(1)} %get-tuple-element.385) | copy-start | bytes 12292
  446.8 4.8 %copy-start.29 = (f32[1024]{0:T(1024)}, f32[1024]{0:T(1024)S(1)}, u32[]{:S(2)}) copy-start(f32[1024]{0:T(1024)S(1)} %get-tuple-element.384) | copy-start | bytes 12292
Sparse Core Ops, SparseCore 0:
  50.1 155.4 all-gather.18
  208.9 104.5 all-reduce.8
  341.9 39.1 all-reduce.10
  383.1 36.0 all-gather.20

commit v3 on v2

--- a/solution.py
+++ b/solution.py
@@ -26,15 +26,27 @@
     return centered * lax.rsqrt(variance + LN_EPS) * gamma + beta
 
 
-def over_rows(rows, unrolled, step, carry):
-    full = rows // ROW_CHUNK
-    if unrolled:
-        for i in range(full):
-            carry = step(i * ROW_CHUNK, ROW_CHUNK, carry)
-    else:
-        carry = lax.fori_loop(0, full, lambda i, c: step(pl.multiple_of(i * ROW_CHUNK, ROW_CHUNK), ROW_CHUNK, c), carry)
-    if rows % ROW_CHUNK:
-        carry = step(full * ROW_CHUNK, rows % ROW_CHUNK, carry)
+def two_stage(rows, make, use, carry):
+    full, tail = rows // ROW_CHUNK, rows % ROW_CHUNK
+    make(0, ROW_CHUNK, 0)
+
+    def pair(i, carry):
+        for half in range(2):
+            start = pl.multiple_of(i * (2 * ROW_CHUNK) + half * ROW_CHUNK, ROW_CHUNK)
+            make(start + ROW_CHUNK, ROW_CHUNK, 1 - half)
+            carry = use(start, ROW_CHUNK, half, carry)
+        return carry
+
+    pairs = (full - 1) // 2
+    carry = lax.fori_loop(0, pairs, pair, carry)
+    for j in range(2 * pairs, full):
+        if j + 1 < full:
+            make((j + 1) * ROW_CHUNK, ROW_CHUNK, (j + 1) % 2)
+        elif tail:
+            make(full * ROW_CHUNK, tail, full % 2)
+        carry = use(j * ROW_CHUNK, ROW_CHUNK, j % 2, carry)
+    if tail:
+        carry = use(full * ROW_CHUNK, tail, full % 2, carry)
     return carry
 
 
@@ -130,18 +142,23 @@
     return out.reshape(batch, seq_len, width)
 
 
-def logits_kernel(unrolled, which_ref, t_ref, embed_ref, bias_ref, lab_ref, z_ref, stat_ref):
+def logits_kernel(which_ref, t_ref, embed_ref, bias_ref, lab_ref, z_ref, stat_ref, even_ref, odd_ref, t_scr):
     del which_ref
-    t_blk = t_ref[...].astype(jnp.bfloat16)
+    t_scr[...] = t_ref[...].astype(jnp.bfloat16)
     lab = lab_ref[...]
-    cols = t_blk.shape[0]
-
-    def step(start, size, carry):
-        top, total, target = carry
+    cols = t_scr.shape[0]
+    held = (even_ref, odd_ref)
+
+    def make(start, size, slot):
         rows = pl.ds(start, size)
-        z = lax.dot_general(embed_ref[rows, :], t_blk, (((1,), (1,)), ((), ())), preferred_element_type=jnp.float32)
+        z = lax.dot_general(embed_ref[rows, :], t_scr[...], (((1,), (1,)), ((), ())), preferred_element_type=jnp.float32)
         z = z + bias_ref[rows, :]
         z_ref[rows, :] = z
+        held[slot][0:size, :] = z
+
+    def use(start, size, slot, carry):
+        top, total, target = carry
+        z = held[slot][0:size, :]
         new_top = jnp.maximum(top, jnp.max(z, axis=0, keepdims=True))
         total = total * jnp.exp(top - new_top) + jnp.sum(jnp.exp(z - new_top), axis=0, keepdims=True)
         hot = lab - start == lax.broadcasted_iota(jnp.int32, (size, cols), 0)
@@ -150,7 +167,7 @@
 
     zero = jnp.zeros((1, cols), jnp.float32)
     first = (jnp.full((1, cols), -jnp.inf, jnp.float32), zero, zero)
-    top, total, target = over_rows(embed_ref.shape[0], unrolled, step, first)
+    top, total, target = two_stage(embed_ref.shape[0], make, use, first)
     stat_ref[0:1, :] = top
     stat_ref[1:2, :] = total
     stat_ref[2:3, :] = target
@@ -163,12 +180,12 @@
     return lambda k, which: lax.rem(which[0] + 1 + k // per_plane, planes) * per_plane + lax.rem(k, per_plane)
 
 
-def logits_call(unrolled, which, t_rows, embed, bias_col, lab_row, planes, per_plane):
+def logits_call(which, t_rows, embed, bias_col, lab_row, planes, per_plane):
     slots = lab_row.shape[1]
     vocab, width = embed.shape
     where = block_map(planes, per_plane)
     return pl.pallas_call(
-        functools.partial(logits_kernel, unrolled),
+        logits_kernel,
         grid_spec=pltpu.PrefetchScalarGridSpec(
             num_scalar_prefetch=1,
             grid=(slots // BLOCK_N,),
@@ -182,6 +199,7 @@
                 pl.BlockSpec((vocab, BLOCK_N), lambda k, which: (0, k)),
                 pl.BlockSpec((8, BLOCK_N), lambda k, which: (0, k)),
             ],
+            scratch_shapes=[pltpu.VMEM((ROW_CHUNK, BLOCK_N), jnp.float32)] * 2 + [pltpu.VMEM((BLOCK_N, width), jnp.bfloat16)],
         ),
         out_shape=[jax.ShapeDtypeStruct((vocab, slots), jnp.float32), jax.ShapeDtypeStruct((8, slots), jnp.float32)],
         compiler_params=params(),
@@ -196,23 +214,27 @@
     return jnp.where(hot, soft - 1.0, soft) * stat_ref[2:3, :]
 
 
-def dt_kernel(unrolled, z_ref, stat_ref, lab_ref, embed_ref, dt_ref):
+def dt_kernel(z_ref, stat_ref, lab_ref, embed_ref, dt_ref, even_ref, odd_ref):
     lab = lab_ref[...]
-
-    def step(start, size, acc):
-        rows = pl.ds(start, size)
-        dz = dz_of(z_ref[rows, :], stat_ref, lab, start).astype(jnp.bfloat16)
-        return acc + lax.dot_general(dz, embed_ref[rows, :], (((0,), (0,)), ((), ())), preferred_element_type=jnp.float32)
-
-    dt_ref[...] = over_rows(embed_ref.shape[0], unrolled, step, jnp.zeros(dt_ref.shape, jnp.float32))
-
-
-def dt_call(unrolled, z, stat, lab_row, embed):
+    held = (even_ref, odd_ref)
+    dt_ref[...] = jnp.zeros_like(dt_ref)
+
+    def make(start, size, slot):
+        held[slot][0:size, :] = dz_of(z_ref[pl.ds(start, size), :], stat_ref, lab, start).astype(jnp.bfloat16)
+
+    def use(start, size, slot, carry):
+        dt_ref[...] += lax.dot_general(held[slot][0:size, :], embed_ref[pl.ds(start, size), :], (((0,), (0,)), ((), ())), preferred_element_type=jnp.float32)
+        return carry
+
+    two_stage(embed_ref.shape[0], make, use, 0)
+
+
+def dt_call(z, stat, lab_row, embed):
     slots = z.shape[1]
     vocab, width = embed.shape
     block = DT_BLOCK
     return pl.pallas_call(
-        functools.partial(dt_kernel, unrolled),
+        dt_kernel,
         grid=(slots // block,),
         in_specs=[
             pl.BlockSpec((vocab, block), lambda k: (0, k)),
@@ -222,18 +244,19 @@
         ],
         out_specs=pl.BlockSpec((block, width), lambda k: (k, 0)),
         out_shape=jax.ShapeDtypeStruct((slots, width), jnp.float32),
+        scratch_shapes=[pltpu.VMEM((ROW_CHUNK, block), jnp.bfloat16)] * 2,
         compiler_params=params(),
         cost_estimate=pl.CostEstimate(flops=2 * slots * vocab * width, bytes_accessed=slots * vocab * 4, transcendentals=slots * vocab),
         name="dt",
     )(z, stat, lab_row, embed)
 
 
-def de_kernel(unrolled, first, part, which_ref, z_ref, stat_ref, lab_ref, t_ref, *rest):
+def de_kernel(first, part, which_ref, z_ref, stat_ref, lab_ref, t_ref, *rest):
     del which_ref
     if first:
-        de_out, db_out, de_ref, db_ref, sems = rest
+        de_out, db_out, de_ref, db_ref, t_scr, even_ref, odd_ref, sems = rest
     else:
-        de_in, db_in, de_out, db_out, de_ref, db_ref, sems = rest
+        de_in, db_in, de_out, db_out, de_ref, db_ref, t_scr, even_ref, odd_ref, sems = rest
     k = pl.program_id(0)
     part_rows = de_ref.shape[0]
     here = pl.ds(part * part_rows, part_rows)
@@ -252,19 +275,23 @@
             two.wait()
 
     lab = lab_ref[...] - part * part_rows
-    t_blk = t_ref[...].astype(jnp.bfloat16)
-
-    def step(start, size, carry):
+    t_scr[...] = t_ref[...].astype(jnp.bfloat16)
+    held = (even_ref, odd_ref)
+
+    def make(start, size, slot):
         rows = pl.ds(start, size)
         dz = dz_of(z_ref[rows, :], stat_ref, lab, start)
         lanes = dz[:, 0:128]
         for c in range(128, dz.shape[1], 128):
             lanes = lanes + dz[:, c:c + 128]
         db_ref[rows, :] += lanes
-        de_ref[rows, :] += jnp.dot(dz.astype(jnp.bfloat16), t_blk, preferred_element_type=jnp.float32)
+        held[slot][0:size, :] = dz.astype(jnp.bfloat16)
+
+    def use(start, size, slot, carry):
+        de_ref[pl.ds(start, size), :] += jnp.dot(held[slot][0:size, :], t_scr[...], preferred_element_type=jnp.float32)
         return carry
 
-    over_rows(part_rows, unrolled, step, 0)
+    two_stage(part_rows, make, use, 0)
 
     @pl.when(k == pl.num_programs(0) - 1)
     def _():
@@ -276,7 +303,7 @@
         two.wait()
 
 
-def de_call(unrolled, which, z, stat, lab_row, t_rows, planes, per_plane, carry=None, part=0, parts=1):
+def de_call(which, z, stat, lab_row, t_rows, planes, per_plane, carry=None, part=0, parts=1):
     vocab, slots = z.shape
     width = t_rows.shape[1]
     where = block_map(planes, per_plane)
@@ -295,13 +322,15 @@
         args += list(carry)
         aliases = {5: 0, 6: 1}
     return pl.pallas_call(
-        functools.partial(de_kernel, unrolled, first, part),
+        functools.partial(de_kernel, first, part),
         grid_spec=pltpu.PrefetchScalarGridSpec(
             num_scalar_prefetch=1,
             grid=(slots // BLOCK_N,),
             in_specs=in_specs,
             out_specs=[pl.BlockSpec(memory_space=pl.ANY), pl.BlockSpec(memory_space=pl.ANY)],
-            scratch_shapes=[pltpu.VMEM((part_rows, width), jnp.float32), pltpu.VMEM((part_rows, 128), jnp.float32), pltpu.SemaphoreType.DMA((2,))],
+            scratch_shapes=[pltpu.VMEM((part_rows, width), jnp.float32), pltpu.VMEM((part_rows, 128), jnp.float32), pltpu.VMEM((BLOCK_N, width), jnp.bfloat16)]
+            + [pltpu.VMEM((ROW_CHUNK, BLOCK_N), jnp.bfloat16)] * 2
+            + [pltpu.SemaphoreType.DMA((2,))],
         ),
         out_shape=[jax.ShapeDtypeStruct((vocab, width), jnp.float32), jax.ShapeDtypeStruct((vocab, 128), jnp.float32)],
         input_output_aliases=aliases,
@@ -326,51 +355,54 @@
     return jnp.sum(jnp.where(hot, values[..., None, :], 0), axis=-1)
 
 
+def earlier_of(batch):
+    return (jnp.arange(batch)[:, None] > jnp.arange(batch)[None, :]).astype(jnp.float32)
+
+
 def solution(mesh):
     dp, tp = mesh.shape["dp"], mesh.shape["tp"]
 
-    def body(unrolled, slots, hidden, positions, weights, small, counts, w_t, b_t, gamma, beta, embed, out_bias):
+    def share_of(slots, hidden, weights, plan, w_t, b_t, gamma, beta):
+        offset, _, _, rowpos_col, seat_row = plan
+        share = slots // tp
+        low = lax.axis_index("tp") * share
+        groups = hidden.shape[0] // GROUP
+        first_of = offset.reshape(groups, GROUP)[:, 0]
+        ends = first_of + jnp.sum(weights.reshape(groups, -1), axis=1).astype(jnp.int32)
+        bounds = jnp.sum(jnp.stack([ends <= low, first_of < low + share]).astype(jnp.int32), axis=1)
+        some = pick(hidden, rowpos_col, seat_row, bounds, offset, slots)
+        part_rows = lax.dynamic_slice_in_dim(some, low, share, 0)
+        pre_act = jnp.dot(part_rows, w_t, preferred_element_type=jnp.float32) + b_t
+        return lax.optimization_barrier(gelu_norm(pre_act, gamma, beta).astype(jnp.bfloat16).astype(jnp.float32))
+
+    def body(slots, sent, hidden, positions, weights, turned, plan, w_t, b_t, gamma, beta, embed, out_bias):
         batch, seq_len, width = hidden.shape
         max_pred = positions.shape[1]
         shard_vocab = embed.shape[0]
         groups = batch // GROUP
-        share = slots // tp
         per_plane = slots // BLOCK_N
         dp_idx, tp_idx = lax.axis_index("dp"), lax.axis_index("tp")
         which = dp_idx.reshape(1).astype(jnp.int32)
-        denom = jnp.sum(counts).astype(jnp.float32) + LOSS_EPS
-
-        column = jnp.arange(max_pred, dtype=jnp.int32)
-        before = (jnp.arange(batch)[:, None] > jnp.arange(batch)[None, :]).astype(jnp.float32)
-        by_seq = jnp.sum(weights, axis=1)
-        offset = jnp.sum(before * by_seq[None, :], axis=1).astype(jnp.int32)
-        seat = jnp.where(weights > 0, offset[:, None] + column, -WINDOW * batch)
-        first_of = offset.reshape(groups, GROUP)[:, 0]
-        ends = first_of + jnp.sum(by_seq.reshape(groups, GROUP), axis=1).astype(jnp.int32)
-        row_of = positions + (jnp.arange(batch, dtype=jnp.int32) % GROUP * seq_len)[:, None]
-        rowpos_col = row_of.reshape(-1, 1)
-        seat_row = seat.reshape(groups, 1, -1)
-
-        def transform(rows):
-            pre_act = jnp.dot(rows, w_t, preferred_element_type=jnp.float32) + b_t
-            return gelu_norm(pre_act, gamma, beta).astype(jnp.bfloat16)
-
-        low = tp_idx * share
-        bounds = jnp.sum(jnp.stack([ends <= low, first_of < low + share]).astype(jnp.int32), axis=1)
-        some = pick(hidden, rowpos_col, seat_row, bounds, offset, slots)
-        part_rows = lax.dynamic_slice_in_dim(some, low, share, 0)
-        t_part = lax.optimization_barrier(transform(part_rows).astype(jnp.float32))
+        denom = jnp.sum(turned[:, 1]) + LOSS_EPS
+        offset, seat, row_of, rowpos_col, seat_row = plan
+        before, column = earlier_of(batch), jnp.arange(max_pred, dtype=jnp.int32)
+
+        t_part = share_of(slots, hidden, weights, plan, w_t, b_t, gamma, beta) if sent is None else sent
         t_all = lax.all_gather(t_part, ("dp", "tp"), axis=0, tiled=True)
 
-        small, held, bias_col, t_part = lax.optimization_barrier((small, hidden, out_bias, t_part))
+        turned, held, bias_col, t_part = lax.optimization_barrier((turned, hidden, out_bias, t_part))
         bias_col = bias_col.reshape(-1, 1)
         every = jnp.array([0, groups], jnp.int32)
         tok_rows = pick(held, rowpos_col, seat_row, every, offset, slots)
         pre_act = jnp.dot(tok_rows, w_t, preferred_element_type=jnp.float32) + b_t
-        normed, norm_vjp = jax.vjp(gelu_norm, pre_act, gamma, beta)
-        t_own = normed.astype(jnp.bfloat16)
-
-        turned = lax.dynamic_slice_in_dim(jnp.concatenate([small, small]), dp_idx, dp, 0)
+        activated, gelu_vjp = jax.vjp(lambda u: jax.nn.gelu(u, approximate=False), pre_act)
+        slope = gelu_vjp(jnp.ones_like(pre_act))[0]
+        centered = activated - jnp.mean(activated, axis=-1, keepdims=True)
+        spread = lax.rsqrt(jnp.mean(centered * centered, axis=-1, keepdims=True) + LN_EPS)
+        unit = centered * spread
+        t_own = (unit * gamma + beta).astype(jnp.bfloat16)
+        slope, unit = lax.optimization_barrier((slope, unit))
+
         ahead = jnp.sum(jnp.where(before[None] > 0, jnp.sum(turned[:, 1].reshape(dp, 1, batch, max_pred), axis=3), 0.0), axis=2)
         index = jnp.where(turned[:, 1].reshape(dp, batch, max_pred) > 0, ahead[:, :, None].astype(jnp.int32) + column, -1)
         index = index.reshape(dp, batch * max_pred)
@@ -378,45 +410,64 @@
         total = jnp.sum(turned[:, 1], axis=1)
         weight_rows = (jnp.arange(slots, dtype=jnp.int32)[None, :] < total[:, None].astype(jnp.int32)).astype(jnp.float32)
         own_lab = packed(labels[:1], index[:1], slots)
-        z_own, stat_own = logits_call(unrolled, which, t_own, embed, bias_col, own_lab, 0, per_plane)
+        z_own, stat_own = logits_call(which, t_own, embed, bias_col, own_lab, 0, per_plane)
         rows_own, ce = combine(stat_own, weight_rows[0], denom)
-        dt_part = dt_call(unrolled, z_own, rows_own, own_lab, embed)
+        dt_part = dt_call(z_own, rows_own, own_lab, embed)
         d_normed = lax.psum(dt_part, "tp")
-        carry = de_call(unrolled, which, z_own, rows_own, own_lab, t_own, 0, per_plane)
+        carry = de_call(which, z_own, rows_own, own_lab, t_own, 0, per_plane)
         far_lab = packed(labels[1:], index[1:], slots).reshape(1, -1)
         loss = jnp.sum(weight_rows[0] * ce)
 
         t_all, carry, far_lab = lax.optimization_barrier((t_all, carry, far_lab))
-        z_far, stat_far = logits_call(unrolled, which, t_all, embed, bias_col, far_lab, dp, per_plane)
+        z_far, stat_far = logits_call(which, t_all, embed, bias_col, far_lab, dp, per_plane)
         rows_far, _ = combine(stat_far, weight_rows[1:].reshape(-1), denom)
 
-        d_normed, rows_far = lax.optimization_barrier((d_normed, rows_far))
-        d_pre, d_gamma, d_beta = norm_vjp(d_normed)
+        de_sum, db_sum = de_call(which, z_far, rows_far, far_lab, t_all, dp, per_plane, carry)
+
+        d_normed, db_sum = lax.optimization_barrier((d_normed, db_sum))
+        d_unit = d_normed * gamma
+        along = jnp.mean(d_unit * unit, axis=-1, keepdims=True)
+        d_act = (d_unit - jnp.mean(d_unit, axis=-1, keepdims=True) - unit * along) * spread
+        d_pre = d_act * slope
+        d_gamma = jnp.sum(d_normed * unit, axis=0)
+        d_beta = jnp.sum(d_normed, axis=0)
         d_pre_bf = d_pre.astype(jnp.bfloat16)
-        d_rows = jnp.einsum("ne,de->nd", d_pre_bf, w_t, preferred_element_type=jnp.float32).astype(jnp.bfloat16)
         cut = width // tp
         part_cols = lax.dynamic_slice_in_dim(tok_rows, tp_idx * cut, cut, 1)
         d_w_t = jnp.einsum("nd,ne->de", part_cols, d_pre_bf, preferred_element_type=jnp.float32)
         vecs = [jnp.sum(d_pre, axis=0)[None], d_gamma[None], d_beta[None], jnp.full((5, width), loss)]
-        block = jnp.concatenate([d_w_t] + vecs)
-        d_rows, block, de_sum, db_sum = lax.optimization_barrier((d_rows, block, *carry))
+        block, d_pre_bf = lax.optimization_barrier((jnp.concatenate([d_w_t] + vecs), d_pre_bf))
         block = lax.psum(block, "dp")
-        carry = de_call(unrolled, which, z_far, rows_far, far_lab, t_all, dp, per_plane, (de_sum, db_sum), 0, 2)
-        block, de_sum, db_sum = lax.optimization_barrier((block, *carry))
         d_w_t = lax.all_gather(block[:cut], "tp", axis=0, tiled=True)
-        d_embed, d_bias = de_call(unrolled, which, z_far, rows_far, far_lab, t_all, dp, per_plane, (de_sum, db_sum), 1, 2)
-        d_rows, d_bias = lax.optimization_barrier((d_rows, d_bias))
+        d_rows = jnp.einsum("ne,de->nd", d_pre_bf, w_t, preferred_element_type=jnp.float32).astype(jnp.bfloat16)
         d_hidden = put(d_rows, row_of.reshape(groups, 1, -1), seat.reshape(-1, 1), offset, batch, seq_len)
-        d_out_bias = jnp.sum(d_bias, axis=1)
-        return block[cut + 3, 0] / denom, d_hidden, d_w_t, block[cut], block[cut + 1], block[cut + 2], d_embed, d_out_bias
+        d_out_bias = jnp.sum(db_sum, axis=1)
+        return block[cut + 3, 0] / denom, d_hidden, d_w_t, block[cut], block[cut + 1], block[cut + 2], de_sum, d_out_bias
 
     def local_step(hidden, positions, labels, weights, w_t, b_t, gamma, beta, embed, out_bias):
+        batch, seq_len, _ = hidden.shape
+        groups = batch // GROUP
         small = jnp.stack([labels.reshape(-1).astype(jnp.float32), weights.reshape(-1)])
-        small = lax.all_gather(small, "dp", axis=0)
-        counts = jnp.sum((small[:, 1] > 0).astype(jnp.int32), axis=1)
-        fits = jnp.max(counts) <= PACKED_ROWS
-        args = (hidden, positions, weights, small, counts, w_t, b_t, gamma, beta, embed, out_bias)
-        return lax.cond(fits, functools.partial(body, True, PACKED_ROWS), functools.partial(body, False, labels.size), *args)
+        rings = [[((j + k) % dp, j) for j in range(dp)] for k in range(1, dp)]
+        turned = jnp.stack([small] + [lax.ppermute(small, "dp", ring) for ring in rings])
+
+        column = jnp.arange(weights.shape[1], dtype=jnp.int32)
+        by_seq = jnp.sum(weights, axis=1)
+        offset = jnp.sum(earlier_of(batch) * by_seq[None, :], axis=1).astype(jnp.int32)
+        seat = jnp.where(weights > 0, offset[:, None] + column, -WINDOW * batch)
+        row_of = positions + (jnp.arange(batch, dtype=jnp.int32) % GROUP * seq_len)[:, None]
+        plan = (offset, seat, row_of, row_of.reshape(-1, 1), seat.reshape(groups, 1, -1))
+        sent = share_of(PACKED_ROWS, hidden, weights, plan, w_t, b_t, gamma, beta)
+        fits = jnp.max(jnp.sum(turned[:, 1], axis=1)) <= PACKED_ROWS
+        args = (hidden, positions, weights, turned, plan, w_t, b_t, gamma, beta, embed, out_bias)
+
+        def packed_form(sent, *args):
+            return body(PACKED_ROWS, sent, *args)
+
+        def whole_form(sent, *args):
+            return body(labels.size, None, *args)
+
+        return lax.cond(fits, packed_form, whole_form, sent, *args)
 
     in_specs = (P("dp", None, None), P("dp", None), P("dp", None), P("dp", None), P(None, None), P(None), P(None), P(None), P("tp", None), P("tp"))
     out_specs = (P(), P("dp", None, None), P(None, None), P(None), P(None), P(None), P("tp", None), P("tp"))

time: 469 us -> 473 us (level)
  Pallas kernels: 253 us -> 277 us
  blocking collectives: 38.1 us -> 21.6 us
  waiting for transfers between devices: 48.7 us -> 39.8 us
  starting transfers between devices: 0.46 us -> 6.35 us
    psum x1, waiting for transfers between devices: 4.16 us -> 39.1 us  [body(): block = lax.psum(block, 'dp')]
    psum x1, waiting for transfers between devices: 34.3 us -> 0.02 us  [body(): d_normed = lax.psum(dt_part, 'tp')]
    pallas_call x6 -> x5, Pallas kernels: 199 us -> 224 us  [the longest x2 105 us: de_call(): pl.pallas_call(functools.partial(de_kernel, first, part), grid_spec=pltpu...]
    all_gather x1 -> x0, blocking collectives: 14.9 us -> none  [local_step(): small = lax.all_gather(small, 'dp', axis=0)]
    all_gather x1, waiting for transfers between devices: 10.2 us -> 0.01 us  [body(): t_all = lax.all_gather(t_part, ('dp', 'tp'), axis=0, tiled=True)]
    ppermute x0 -> x3, starting transfers between devices: none -> 6.19 us  [local_step(): lax.ppermute(small, 'dp', ring)]
    reduce_sum x9 -> x10, other arithmetic: 16.4 us -> 15.5 us  [the longest x1 5.84 us: body(): d_gamma = jnp.sum(d_normed * unit, axis=0)]
  transfers between devices with their start and end apart: 4 -> 7, of which waited for: 3 -> 2; matrix products, arithmetic and copies ran while one was open for 10% -> 15% of each run, Pallas kernels for 53% -> 60%
where the time goes in v3:
time: 473 us; the launch traced here: 465 us
  Pallas kernels  277 us (59%)
  waiting for transfers between devices  39.8 us (8%)
  other arithmetic  36.8 us (8%)
  matrix products  33.5 us (7%)
  local copies, waits for them, and re-layouts  29.1 us (6%)
  blocking collectives  21.6 us (5%)
  between operations  15.9 us (3%)
  starting transfers between devices  6.35 us (1%)
  loops' own time  5.24 us (1%)
    pallas_call x2, Pallas kernels, de_call(): pl.pallas_call(functools.partial(de_kernel, first, part), grid_spec=pltpu...  105 us
    pallas_call x2, Pallas kernels, logits_call(): pl.pallas_call(logits_kernel, grid_spec=pltpu.PrefetchScalarGridSpec(num_...  91.5 us
    psum x1, waiting for transfers between devices, body(): block = lax.psum(block, 'dp')  39.1 us
    pallas_call x2, Pallas kernels, pick(): pl.pallas_call(pick_kernel, grid_spec=pltpu.PrefetchScalarGridSpec(num_sc...  31.5 us
    pallas_call x1, Pallas kernels, dt_call(): pl.pallas_call(dt_kernel, grid=(slots // block,), in_specs=[pl.BlockSpec(...  27.3 us
    all_gather x2, blocking collectives, combine(): parts = lax.all_gather(stat[:3], 'tp', axis=0)  21.6 us
    pallas_call x1, Pallas kernels, put(): pl.pallas_call(put_kernel, grid_spec=pltpu.PrefetchScalarGridSpec(num_sca...  21.5 us
    dot_general x1, matrix products, body(): pre_act = jnp.dot(tok_rows, w_t, preferred_element_type=jnp.float32) + b_t  20.6 us
  transfers between devices with their start and end apart: 7, of which 2 were waited for; matrix products, arithmetic and copies ran while one was open for 15% of the time, Pallas kernels for 60%

profile of v3, /device:TPU:0, one launch (start us, length us, event | category | flops | bytes accessed | tf_op | source)
XLA Modules:
  0.0 465.4 jit_solution(3711696248394394885)
XLA Ops:
  7.2 0.7 convert_element_type.144
  8.1 0.8 copy.115
  9.1 4.2 collective-permute-start.1
  13.2 1.3 collective-permute-start
  14.6 0.7 collective-permute-start.2
  15.3 0.7 reduce_sum.437
  16.5 0.8 copy.117
  17.7 0.6 copy.118.seat_ref
  18.3 1.5 copy.119.rowpos_ref
  19.8 0.6 fusion.61.bounds_ref
  20.4 8.1 %pick.7 = bf16[1536,1024]{1,0:T(8,128)(2,1)} custom-call(s32[2]{0:T(128)} %fusion.61.bounds_ref, s32[128]{0:T(128)S(1)} %convert_element_type.147.off_ref, s32[16,1,160]{2,1,0:T(1,128)} %copy.118.seat_ref, s32[2560,1]{1,0:T(8,128)} %copy.119.rowpos_ref, bf16[16384,1024]{1,0:T(8,128)(2,1)} %bitcast.131), custom_call_target="tpu_custom_call" | custom-call | flops 5905580032 | bytes 33554432 | tf_op jit(solution)/shard_map/pick/pallas_call | solution.py:91
  28.6 4.1 fusion.79
  32.7 0.2 multiply_reduce_fusion.11
  33.0 0.2 fusion.59
  33.3 0.1 slice_reduce_fusion.15
  33.4 0.6 reduce_max.45
  34.7 418.0 %conditional.1 = (f32[3824,1024]{1,0:T(8,128)}, f32[]{:T(128)}, bf16[128,128,1024]{2,1,0:T(8,128)(2,1)}, f32[1024,1024]{1,0:T(8,128)}, f32[1024]{0:T(1024)S(1)},...) conditional(s32[]{:T(128)} %convert_element_type.146, (s32[128]{0:T(128)S(1)}, ...), branch_computations={%region_8.36_spmd, %region_36.59_spmd} | conditional | flops 210596691968 | bytes 960796480 | solution.py:470
  38.1 0.8 copy-done.3
  39.0 0.6 copy.124.seat_ref
  39.8 0.3 squeeze.52
  40.8 1.7 select_reduce_fusion.4
  42.5 0.6 reduce_sum.414.lab_ref
  43.1 1.5 copy.125.rowpos_ref
  44.6 1.9 reshape.547.bias_ref
  46.5 23.4 %pick.6 = bf16[1536,1024]{1,0:T(8,128)(2,1)} custom-call(s32[2]{0:T(128)S(1)} %get-tuple-element.96.bounds_ref, s32[128]{0:T(128)S(1)} %get-tuple-element.97.off_ref, s32[16,1,160]{2,1,0:T(1,128)} %copy.124.seat_ref, s32[2560,1]{1,0:T(8,128)} %copy.125.rowpos_ref, bf16[16384,1024]{1,0:T(8,128)(2,1)} %bitcast.134), custom_call_target="tpu_custom_call" | custom-call | flops 5905580032 | bytes 33554432 | tf_op jit(solution)/shard_map/cond/branch_1_fun/pick/pallas_call | solution.py:91
  69.8 20.6 %multiply_add_fusion.1 = (f32[1536,1024]{1,0:T(8,128)}, f32[1536,1024]{1,0:T(8,128)S(1)}, f32[1536,1024]{1,0:T(8,128)}) fusion(f32[1024]{0:T(1024)S(1)} %get-tuple-element.106, bf16[1536,1024]{1,0:T(8,128)(2,1)} %pick.6, bf16[1024,1024]{1,0:T(8,128)(2,1)} %get-tuple-element.105), kind=kOutput, calls=%fused_computation.110 | convolution fusion | flops 3329753088 | bytes 24121344 | tf_op jit(solution)/shard_map/cond/branch_1_fun/dot_general | solution.py:397
  90.4 3.8 fusion.71
  94.3 0.8 multiply_reduce_fusion.8
  95.1 4.3 add_convert_fusion.3
  99.4 26.1 %logits.6 = (f32[3824,1536]{1,0:T(8,128)}, f32[8,1536]{1,0:T(8,128)}) custom-call(s32[1]{0:T(128)} %bitcast.17.which_ref, bf16[1536,1024]{1,0:T(8,128)(2,1)} %get-tuple-element.261.t_ref, bf16[3824,1024]{1,0:T(8,128)(2,1)} %get-tuple-element.109.embed_ref, f32[3824,1]{1,0:T(8,128)} %reshape.547.bias_ref, s32[1,1536]{1,0:T(1,128)} %reduce_sum.414.lab_ref), custom_call_target="tpu_custom_call" | custom-call | flops 12029263872 | bytes 23494656 | tf_op jit(solution)/shard_map/cond/branch_1_fun/logits/pallas_call | solution.py:187
  125.4 0.8 slice_bitcast_fusion.5
  126.2 9.9 %all-gather.6 = f32[8,3,1536]{2,1,0:T(4,128)S(1)} all-gather(f32[1,3,1536]{2,1,0:T(4,128)S(1)} %slice_bitcast_fusion.5), channel_id=4, replica_groups=mesh['dp'=4,'tp'=8] {'tp'}, dimensions={0}, use_global_device_ids=true | all-gather | bytes 165888 | tf_op jit(solution)/shard_map/cond/branch_1_fun/all_gather | solution.py:344
  136.2 0.1 fusion.78
  136.3 0.6 slice_reduce_fusion.9
  137.7 0.6 multiply_reduce_fusion.10
  138.4 0.7 stack.33.stat_ref
  139.1 27.3 %dt.3 = f32[1536,1024]{1,0:T(8,128)} custom-call(f32[3824,1536]{1,0:T(8,128)} %get-tuple-element.112.z_ref, f32[8,1536]{1,0:T(8,128)} %stack.33.stat_ref, s32[1,1536]{1,0:T(1,128)} %reduce_sum.414.lab_ref, bf16[3824,1024]{1,0:T(8,128)(2,1)} %get-tuple-element.109.embed_ref), custom_call_target="tpu_custom_call" | custom-call | flops 12029263872 | bytes 23494656 | tf_op jit(solution)/shard_map/cond/branch_1_fun/dt/pallas_call | solution.py:236
  166.5 30.0 %de.6 = (f32[3824,1024]{1,0:T(8,128)}, f32[3824,128]{1,0:T(8,128)}) custom-call(s32[1]{0:T(128)} %bitcast.17.which_ref, f32[3824,1536]{1,0:T(8,128)} %get-tuple-element.112.z_ref, f32[8,1536]{1,0:T(8,128)} %stack.33.stat_ref, s32[1,1536]{1,0:T(1,128)} %reduce_sum.414.lab_ref, bf16[1536,1024]{1,0:T(8,128)(2,1)} %get-tuple-element.261.t_ref), custom_call_target="tpu_custom_call" | custom-call | flops 12029263872 | bytes 23494656 | tf_op jit(solution)/shard_map/cond/branch_1_fun/de/pallas_call | solution.py:324
  196.6 0.2 eq.74
  196.7 5.8 %select_reduce_fusion.3 = s32[3,1536]{1,0:T(4,128)S(1)} fusion(s32[3,2560]{1,0:T(4,128)S(1)} %slice_bitcast_fusion.4, s32[3,2560]{1,0:T(4,128)S(1)} %eq.74), kind=kLoop, calls=%fused_computation.101 | loop fusion | flops 35384832 | bytes 79872 | tf_op jit(solution)/shard_map/cond/branch_1_fun/reduce_sum | solution.py:355
  202.5 0.6 copy.140
  203.2 65.4 %logits.7 = (f32[3824,4608]{1,0:T(8,128)}, f32[8,4608]{1,0:T(8,128)}) custom-call(s32[1]{0:T(128)} %bitcast.17.which_ref, f32[6144,1024]{1,0:T(8,128)} %all-gather.17.cloned.1.call-done.t_ref, bf16[3824,1024]{1,0:T(8,128)(2,1)} %get-tuple-element.109.embed_ref, f32[3824,1]{1,0:T(8,128)} %reshape.547.bias_ref, s32[1,4608]{1,0:T(1,128)} %bitcast.148), custom_call_target="tpu_custom_call" | custom-call | flops 36087791616 | bytes 70483968 | tf_op jit(solution)/shard_map/cond/branch_1_fun/logits/pallas_call | solution.py:187
  268.6 0.9 slice_bitcast_fusion.3
  269.5 11.7 %all-gather.7 = f32[8,3,4608]{2,1,0:T(4,128)S(1)} all-gather(f32[1,3,4608]{2,1,0:T(4,128)S(1)} %slice_bitcast_fusion.3), channel_id=5, replica_groups=mesh['dp'=4,'tp'=8] {'tp'}, dimensions={0}, use_global_device_ids=true | all-gather | bytes 497664 | tf_op jit(solution)/shard_map/cond/branch_1_fun/all_gather | solution.py:344
  281.2 0.3 fusion.76
  281.6 0.8 stack.35.stat_ref
  282.4 75.3 %de.7 = (f32[3824,1024]{1,0:T(8,128)}, f32[3824,128]{1,0:T(8,128)}) custom-call(s32[1]{0:T(128)} %bitcast.17.which_ref, f32[3824,4608]{1,0:T(8,128)} %get-tuple-element.118.z_ref, f32[8,4608]{1,0:T(8,128)} %stack.35.stat_ref, s32[1,4608]{1,0:T(1,128)} %bitcast.149, ...), custom_call_target="tpu_custom_call", output_to_operand_aliasing={{0}: (5, {}), {1}: (6, {})} | custom-call | flops 36087791616 | bytes 70483968 | tf_op jit(solution)/shard_map/cond/branch_1_fun/de/pallas_call | solution.py:324
  357.8 5.8 %multiply_reduce_fusion.6 = (f32[1024]{0:T(1024)S(1)}, f32[1536]{0:T(1024)S(1)}, f32[1536]{0:T(1024)S(1)}, f32[1024]{0:T(1024)S(1)}) fusion(f32[1536,1024]{1,0:T(8,128)} %all-reduce.9.cloned.1.call-done, f32[1536,1024]{1,0:T(8,128)} %get-tuple-element.124, f32[1024]{0:T(1024)S(1)} %get-tuple-element.107), kind=kLoop, calls=%fused_computation.107 | loop fusion | flops 11004928 | bytes 12607488 | tf_op jit(solution)/shard_map/cond/branch_1_fun/reduce_sum | solution.py:432
  363.6 0.6 copy-done.1
  364.2 5.6 %fusion.69 = (f32[1024]{0:T(1024)S(1)}, bf16[1536,1024]{1,0:T(8,128)(2,1)S(1)}) fusion(f32[1536,1024]{1,0:T(8,128)} %get-tuple-element.125, f32[1536]{0:T(1024)S(1)} %add_rsqrt_fusion.2, f32[1536,1024]{1,0:T(8,128)} %get-tuple-element.124, f32[1536]{0:T(1024)S(1)} %get-tuple-element.305, f32[1536]{0:T(1024)S(1)} %get-tuple-element.306, ...), kind=kLoop, calls=%fused_computation.215 | loop fusion | flops 12581888 | bytes 22046720 | tf_op jit(solution)/shard_map/cond/branch_1_fun/reduce_sum | solution.py:438
  369.8 2.4 fusion.38
  372.2 0.6 broadcast_in_dim.138
  372.9 2.4 concatenate.5
  375.4 39.1 %all-reduce.11.cloned.1.call-done = f32[136,1024]{1,0:T(8,128)} async-done(((f32[136,1024]{1,0:T(8,128)}), f32[136,1024]{1,0:T(8,128)}) %all-reduce.11.cloned.1.call-update) | async-done | bytes 557072 | tf_op jit(solution)/shard_map/cond/branch_1_fun/psum | solution.py:440
  414.4 1.9 slice.190
  416.4 0.7 reshape.545.rowpos_ref
  417.1 1.5 reshape.544.seat_ref
  418.5 2.7 reduce_sum.427
  421.3 6.4 %convolution_convert_fusion.1.dh_ref = bf16[1536,1024]{1,0:T(8,128)(2,1)} fusion(bf16[1536,1024]{1,0:T(8,128)(2,1)S(1)} %get-tuple-element.129, bf16[1024,1024]{1,0:T(8,128)(2,1)} %get-tuple-element.105), kind=kOutput, calls=%fused_computation.129 | convolution fusion | flops 3222798336 | bytes 8388608 | tf_op jit(solution)/shard_map/cond/branch_1_fun/ne,de->nd/dot_general | solution.py:442
  427.7 21.5 %put.3 = bf16[16384,1024]{1,0:T(8,128)(2,1)} custom-call(s32[128]{0:T(128)S(1)} %copy-done.26, s32[2560,1]{1,0:T(8,128)} %reshape.544.seat_ref, s32[16,1,160]{2,1,0:T(1,128)} %reshape.545.rowpos_ref, bf16[1536,1024]{1,0:T(8,128)(2,1)} %convolution_convert_fusion.1.dh_ref), custom_call_target="tpu_custom_call" | custom-call | flops 5905580032 | bytes 33554432 | tf_op jit(solution)/shard_map/cond/branch_1_fun/put/pallas_call | solution.py:125
  449.1 1.2 slice.189
  451.0 0.9 fusion.77
  451.9 0.7 all-gather.19.cloned.1.call-done
  452.7 4.8 %copy.199 = f32[1024,1024]{1,0:T(8,128)} copy(f32[1024,1024]{1,0:T(8,128)} %get-tuple-element.345) | data formatting | bytes 8388608
  (99 shorter events, 2.7 us)
Async XLA Ops:
  9.1 24.1 %collective-permute-start.1 = (f32[2,2560]{1,0:T(2,128)S(1)}, f32[2,2560]{1,0:T(2,128)S(1)}, u32[]{:S(2)}, u32[]{:S(2)}) collective-permute-start(f32[2,2560]{1,0:T(2,128)S(1)} %get-tuple-element.308), channel_id=1, source_target_pairs={{16,0},{24,8},{0,16},{8,24},{17,1},{25,9},{1,17},{9,25},{18,2},{26... | collective-permute-start | bytes 61448 | tf_op jit(solution)/shard_map/ppermute | solution.py:452
  13.2 20.0 %collective-permute-start = (f32[2,2560]{1,0:T(2,128)S(1)}, f32[2,2560]{1,0:T(2,128)S(1)}, u32[]{:S(2)}, u32[]{:S(2)}) collective-permute-start(f32[2,2560]{1,0:T(2,128)S(1)} %get-tuple-element.308), channel_id=1, source_target_pairs={{8,0},{16,8},{24,16},{0,24},{9,1},{17,9},{25,17},{1,25},{10,2},{18... | collective-permute-start | bytes 61448 | tf_op jit(solution)/shard_map/ppermute | solution.py:452
  14.6 18.6 %collective-permute-start.2 = (f32[2,2560]{1,0:T(2,128)S(1)}, f32[2,2560]{1,0:T(2,128)S(1)}, u32[]{:S(2)}, u32[]{:S(2)}) collective-permute-start(f32[2,2560]{1,0:T(2,128)S(1)} %get-tuple-element.308), channel_id=1, source_target_pairs={{24,0},{0,8},{8,16},{16,24},{25,1},{1,9},{9,17},{17,25},{26,2},{2,... | collective-permute-start | bytes 61448 | tf_op jit(solution)/shard_map/ppermute | solution.py:452
  17.4 11.1 %copy-start.6 = (s32[128,20]{1,0:T(8,128)}, s32[128,20]{1,0:T(8,128)S(1)}, u32[]{:S(2)}) copy-start(s32[128,20]{1,0:T(8,128)S(1)} %get-tuple-element.314) | copy-start | bytes 30724
  17.5 11.1 %copy-start.9 = (s32[128,20]{1,0:T(8,128)}, s32[128,20]{1,0:T(8,128)S(1)}, u32[]{:S(2)}) copy-start(s32[128,20]{1,0:T(8,128)S(1)} %get-tuple-element.313) | copy-start | bytes 30724
  20.4 8.1 %copy-start.27 = (f32[1024]{0:T(1024)S(1)}, f32[1024]{0:T(1024)}, u32[]{:S(2)}) copy-start(f32[1024]{0:T(1024)} %param.19) | copy-start | bytes 12292
  28.6 4.4 copy-start.12
  28.6 4.4 copy-start.22
  28.6 6.1 %copy-start.20 = (f32[128,20]{0,1:T(8,128)S(1)}, f32[128,20]{0,1:T(8,128)}, u32[]{:S(2)}) copy-start(f32[128,20]{0,1:T(8,128)} %param.17) | copy-start | bytes 30724
  28.6 6.1 %copy-start.21 = (f32[3824]{0:T(1024)S(1)}, f32[3824]{0:T(1024)}, u32[]{:S(2)}) copy-start(f32[3824]{0:T(1024)} %param.23) | copy-start | bytes 45892
  38.0 0.9 copy-start.3
  38.0 31.8 %copy-start.25 = (s32[128]{0:T(128)}, s32[128]{0:T(128)S(1)}, u32[]{:S(2)}) copy-start(s32[128]{0:T(128)S(1)} %get-tuple-element.97.off_ref) | copy-start | bytes 1540 | tf_op jit(solution)/shard_map/cond
  38.1 319.7 %copy-start.15 = (f32[1024]{0:T(1024)}, f32[1024]{0:T(1024)S(1)}, u32[]{:S(2)}) copy-start(f32[1024]{0:T(1024)S(1)} %get-tuple-element.107) | copy-start | bytes 12292 | tf_op jit(solution)/shard_map/cond
  38.1 165.1 %all-gather.17.cloned.1.call-start = ((), (), s32[]{:S(2)}) async-start(), calls=%async_computation.5 | async-start | bytes 25952256 | tf_op jit(solution)/shard_map/cond/branch_1_fun/all_gather | solution.py:391
  38.9 318.8 %all-reduce.9.cloned.1.call-start = ((), (), s32[]{:S(2)}) async-start(), calls=%async_computation.4 | async-start | bytes 12582912 | tf_op jit(solution)/shard_map/cond/branch_1_fun/psum | solution.py:416
  40.6 125.9 %copy-start.4 = (s32[4,128,20]{2,1,0:T(8,128)}, s32[4,128,20]{2,1,0:T(8,128)S(1)}, u32[]{:S(2)}) copy-start(s32[4,128,20]{2,1,0:T(8,128)S(1)} %add_select_fusion.1) | copy-start | bytes 122884 | tf_op jit(solution)/shard_map/cond
  166.4 248.0 %all-reduce.11.cloned.1.call-start = ((), (), s32[]{:S(2)}) async-start(), calls=%async_computation.6 | async-start | bytes 1114112 | tf_op jit(solution)/shard_map/cond/branch_1_fun/psum | solution.py:440
  166.5 30.1 %slice-start.3 = ((s32[4,128,20]{2,1,0:T(8,128)}), s32[3,128,20]{2,1,0:T(8,128)S(1)}, s32[]{:S(2)}) async-start(s32[4,128,20]{2,1,0:T(8,128)} %copy-done.4), calls=%async_computation.11 | async-start | bytes 393216 | tf_op jit(solution)/shard_map/cond/branch_1_fun/slice | solution.py:418
  357.7 6.4 %copy-start.1 = (f32[1536,1024]{1,0:T(8,128)S(1)}, f32[1536,1024]{1,0:T(8,128)}, u32[]{:S(2)}) copy-start(f32[1536,1024]{1,0:T(8,128)} %all-reduce.9.cloned.1.call-done) | copy-start | bytes 18874372 | tf_op jit(solution)/shard_map/cond
  369.8 46.6 %copy-start.8 = (s32[128,20]{1,0:T(8,128)S(1)}, s32[128,20]{1,0:T(8,128)}, u32[]{:S(2)}) copy-start(s32[128,20]{1,0:T(8,128)} %get-tuple-element.128) | copy-start | bytes 30724 | tf_op jit(solution)/shard_map/cond
  369.8 47.3 %copy-start.11 = (s32[128,20]{1,0:T(8,128)S(1)}, s32[128,20]{1,0:T(8,128)}, u32[]{:S(2)}) copy-start(s32[128,20]{1,0:T(8,128)} %get-tuple-element.127) | copy-start | bytes 30724 | tf_op jit(solution)/shard_map/cond
  375.3 77.2 %all-gather.19.cloned.1.call-start = ((), (), s32[]{:S(2)}) async-start(), calls=%async_computation.7 | async-start | bytes 4718592 | tf_op jit(solution)/shard_map/cond/branch_1_fun/all_gather | solution.py:441
  421.3 6.4 %copy-start.26 = (s32[128]{0:T(128)S(1)}, s32[128]{0:T(128)}, u32[]{:S(2)}) copy-start(s32[128]{0:T(128)} %copy-done.25) | copy-start | bytes 1540 | tf_op jit(solution)/shard_map/cond
  452.7 4.8 %copy-start.28 = (f32[1024]{0:T(1024)}, f32[1024]{0:T(1024)S(1)}, u32[]{:S(2)}) copy-start(f32[1024]{0:T(1024)S(1)} %get-tuple-element.348) | copy-start | bytes 12292
  452.7 4.8 %copy-start.29 = (f32[1024]{0:T(1024)}, f32[1024]{0:T(1024)S(1)}, u32[]{:S(2)}) copy-start(f32[1024]{0:T(1024)S(1)} %get-tuple-element.347) | copy-start | bytes 12292
  452.7 4.8 %copy-start.30 = (f32[1024]{0:T(1024)}, f32[1024]{0:T(1024)S(1)}, u32[]{:S(2)}) copy-start(f32[1024]{0:T(1024)S(1)} %get-tuple-element.346) | copy-start | bytes 12292
Sparse Core Ops, SparseCore 0:
  41.7 154.9 all-gather.16
  200.0 103.4 all-reduce.8
  375.4 38.9 all-reduce.10
  416.5 36.0 all-gather.18

commit v4 on v2

--- a/solution.py
+++ b/solution.py
@@ -326,51 +326,54 @@
     return jnp.sum(jnp.where(hot, values[..., None, :], 0), axis=-1)
 
 
+def earlier_of(batch):
+    return (jnp.arange(batch)[:, None] > jnp.arange(batch)[None, :]).astype(jnp.float32)
+
+
 def solution(mesh):
     dp, tp = mesh.shape["dp"], mesh.shape["tp"]
 
-    def body(unrolled, slots, hidden, positions, weights, small, counts, w_t, b_t, gamma, beta, embed, out_bias):
+    def share_of(slots, hidden, weights, plan, w_t, b_t, gamma, beta):
+        offset, _, _, rowpos_col, seat_row = plan
+        share = slots // tp
+        low = lax.axis_index("tp") * share
+        groups = hidden.shape[0] // GROUP
+        first_of = offset.reshape(groups, GROUP)[:, 0]
+        ends = first_of + jnp.sum(weights.reshape(groups, -1), axis=1).astype(jnp.int32)
+        bounds = jnp.sum(jnp.stack([ends <= low, first_of < low + share]).astype(jnp.int32), axis=1)
+        some = pick(hidden, rowpos_col, seat_row, bounds, offset, slots)
+        part_rows = lax.dynamic_slice_in_dim(some, low, share, 0)
+        pre_act = jnp.dot(part_rows, w_t, preferred_element_type=jnp.float32) + b_t
+        return lax.optimization_barrier(gelu_norm(pre_act, gamma, beta).astype(jnp.bfloat16).astype(jnp.float32))
+
+    def body(unrolled, slots, sent, hidden, positions, weights, turned, plan, w_t, b_t, gamma, beta, embed, out_bias):
         batch, seq_len, width = hidden.shape
         max_pred = positions.shape[1]
         shard_vocab = embed.shape[0]
         groups = batch // GROUP
-        share = slots // tp
         per_plane = slots // BLOCK_N
         dp_idx, tp_idx = lax.axis_index("dp"), lax.axis_index("tp")
         which = dp_idx.reshape(1).astype(jnp.int32)
-        denom = jnp.sum(counts).astype(jnp.float32) + LOSS_EPS
-
-        column = jnp.arange(max_pred, dtype=jnp.int32)
-        before = (jnp.arange(batch)[:, None] > jnp.arange(batch)[None, :]).astype(jnp.float32)
-        by_seq = jnp.sum(weights, axis=1)
-        offset = jnp.sum(before * by_seq[None, :], axis=1).astype(jnp.int32)
-        seat = jnp.where(weights > 0, offset[:, None] + column, -WINDOW * batch)
-        first_of = offset.reshape(groups, GROUP)[:, 0]
-        ends = first_of + jnp.sum(by_seq.reshape(groups, GROUP), axis=1).astype(jnp.int32)
-        row_of = positions + (jnp.arange(batch, dtype=jnp.int32) % GROUP * seq_len)[:, None]
-        rowpos_col = row_of.reshape(-1, 1)
-        seat_row = seat.reshape(groups, 1, -1)
-
-        def transform(rows):
-            pre_act = jnp.dot(rows, w_t, preferred_element_type=jnp.float32) + b_t
-            return gelu_norm(pre_act, gamma, beta).astype(jnp.bfloat16)
-
-        low = tp_idx * share
-        bounds = jnp.sum(jnp.stack([ends <= low, first_of < low + share]).astype(jnp.int32), axis=1)
-        some = pick(hidden, rowpos_col, seat_row, bounds, offset, slots)
-        part_rows = lax.dynamic_slice_in_dim(some, low, share, 0)
-        t_part = lax.optimization_barrier(transform(part_rows).astype(jnp.float32))
+        denom = jnp.sum(turned[:, 1]) + LOSS_EPS
+        offset, seat, row_of, rowpos_col, seat_row = plan
+        before, column = earlier_of(batch), jnp.arange(max_pred, dtype=jnp.int32)
+
+        t_part = share_of(slots, hidden, weights, plan, w_t, b_t, gamma, beta) if sent is None else sent
         t_all = lax.all_gather(t_part, ("dp", "tp"), axis=0, tiled=True)
 
-        small, held, bias_col, t_part = lax.optimization_barrier((small, hidden, out_bias, t_part))
+        turned, held, bias_col, t_part = lax.optimization_barrier((turned, hidden, out_bias, t_part))
         bias_col = bias_col.reshape(-1, 1)
         every = jnp.array([0, groups], jnp.int32)
         tok_rows = pick(held, rowpos_col, seat_row, every, offset, slots)
         pre_act = jnp.dot(tok_rows, w_t, preferred_element_type=jnp.float32) + b_t
-        normed, norm_vjp = jax.vjp(gelu_norm, pre_act, gamma, beta)
-        t_own = normed.astype(jnp.bfloat16)
-
-        turned = lax.dynamic_slice_in_dim(jnp.concatenate([small, small]), dp_idx, dp, 0)
+        activated, gelu_vjp = jax.vjp(lambda u: jax.nn.gelu(u, approximate=False), pre_act)
+        slope = gelu_vjp(jnp.ones_like(pre_act))[0]
+        centered = activated - jnp.mean(activated, axis=-1, keepdims=True)
+        spread = lax.rsqrt(jnp.mean(centered * centered, axis=-1, keepdims=True) + LN_EPS)
+        unit = centered * spread
+        t_own = (unit * gamma + beta).astype(jnp.bfloat16)
+        slope, unit = lax.optimization_barrier((slope, unit))
+
         ahead = jnp.sum(jnp.where(before[None] > 0, jnp.sum(turned[:, 1].reshape(dp, 1, batch, max_pred), axis=3), 0.0), axis=2)
         index = jnp.where(turned[:, 1].reshape(dp, batch, max_pred) > 0, ahead[:, :, None].astype(jnp.int32) + column, -1)
         index = index.reshape(dp, batch * max_pred)
@@ -390,33 +393,54 @@
         z_far, stat_far = logits_call(unrolled, which, t_all, embed, bias_col, far_lab, dp, per_plane)
         rows_far, _ = combine(stat_far, weight_rows[1:].reshape(-1), denom)
 
-        d_normed, rows_far = lax.optimization_barrier((d_normed, rows_far))
-        d_pre, d_gamma, d_beta = norm_vjp(d_normed)
+        de_sum, db_sum = de_call(unrolled, which, z_far, rows_far, far_lab, t_all, dp, per_plane, carry, 0, 2)
+
+        d_normed, db_sum = lax.optimization_barrier((d_normed, db_sum))
+        d_unit = d_normed * gamma
+        along = jnp.mean(d_unit * unit, axis=-1, keepdims=True)
+        d_act = (d_unit - jnp.mean(d_unit, axis=-1, keepdims=True) - unit * along) * spread
+        d_pre = d_act * slope
+        d_gamma = jnp.sum(d_normed * unit, axis=0)
+        d_beta = jnp.sum(d_normed, axis=0)
         d_pre_bf = d_pre.astype(jnp.bfloat16)
-        d_rows = jnp.einsum("ne,de->nd", d_pre_bf, w_t, preferred_element_type=jnp.float32).astype(jnp.bfloat16)
         cut = width // tp
         part_cols = lax.dynamic_slice_in_dim(tok_rows, tp_idx * cut, cut, 1)
         d_w_t = jnp.einsum("nd,ne->de", part_cols, d_pre_bf, preferred_element_type=jnp.float32)
         vecs = [jnp.sum(d_pre, axis=0)[None], d_gamma[None], d_beta[None], jnp.full((5, width), loss)]
-        block = jnp.concatenate([d_w_t] + vecs)
-        d_rows, block, de_sum, db_sum = lax.optimization_barrier((d_rows, block, *carry))
+        block, d_pre_bf, de_sum, db_sum = lax.optimization_barrier((jnp.concatenate([d_w_t] + vecs), d_pre_bf, de_sum, db_sum))
         block = lax.psum(block, "dp")
-        carry = de_call(unrolled, which, z_far, rows_far, far_lab, t_all, dp, per_plane, (de_sum, db_sum), 0, 2)
-        block, de_sum, db_sum = lax.optimization_barrier((block, *carry))
+        de_sum, db_sum = de_call(unrolled, which, z_far, rows_far, far_lab, t_all, dp, per_plane, (de_sum, db_sum), 1, 2)
+        block, d_pre_bf, db_sum = lax.optimization_barrier((block, d_pre_bf, db_sum))
         d_w_t = lax.all_gather(block[:cut], "tp", axis=0, tiled=True)
-        d_embed, d_bias = de_call(unrolled, which, z_far, rows_far, far_lab, t_all, dp, per_plane, (de_sum, db_sum), 1, 2)
-        d_rows, d_bias = lax.optimization_barrier((d_rows, d_bias))
+        d_rows = jnp.einsum("ne,de->nd", d_pre_bf, w_t, preferred_element_type=jnp.float32).astype(jnp.bfloat16)
         d_hidden = put(d_rows, row_of.reshape(groups, 1, -1), seat.reshape(-1, 1), offset, batch, seq_len)
-        d_out_bias = jnp.sum(d_bias, axis=1)
-        return block[cut + 3, 0] / denom, d_hidden, d_w_t, block[cut], block[cut + 1], block[cut + 2], d_embed, d_out_bias
+        d_out_bias = jnp.sum(db_sum, axis=1)
+        return block[cut + 3, 0] / denom, d_hidden, d_w_t, block[cut], block[cut + 1], block[cut + 2], de_sum, d_out_bias
 
     def local_step(hidden, positions, labels, weights, w_t, b_t, gamma, beta, embed, out_bias):
+        batch, seq_len, _ = hidden.shape
+        groups = batch // GROUP
         small = jnp.stack([labels.reshape(-1).astype(jnp.float32), weights.reshape(-1)])
-        small = lax.all_gather(small, "dp", axis=0)
-        counts = jnp.sum((small[:, 1] > 0).astype(jnp.int32), axis=1)
-        fits = jnp.max(counts) <= PACKED_ROWS
-        args = (hidden, positions, weights, small, counts, w_t, b_t, gamma, beta, embed, out_bias)
-        return lax.cond(fits, functools.partial(body, True, PACKED_ROWS), functools.partial(body, False, labels.size), *args)
+        rings = [[((j + k) % dp, j) for j in range(dp)] for k in range(1, dp)]
+        turned = jnp.stack([small] + [lax.ppermute(small, "dp", ring) for ring in rings])
+
+        column = jnp.arange(weights.shape[1], dtype=jnp.int32)
+        by_seq = jnp.sum(weights, axis=1)
+        offset = jnp.sum(earlier_of(batch) * by_seq[None, :], axis=1).astype(jnp.int32)
+        seat = jnp.where(weights > 0, offset[:, None] + column, -WINDOW * batch)
+        row_of = positions + (jnp.arange(batch, dtype=jnp.int32) % GROUP * seq_len)[:, None]
+        plan = (offset, seat, row_of, row_of.reshape(-1, 1), seat.reshape(groups, 1, -1))
+        sent = share_of(PACKED_ROWS, hidden, weights, plan, w_t, b_t, gamma, beta)
+        fits = jnp.max(jnp.sum(turned[:, 1], axis=1)) <= PACKED_ROWS
+        args = (hidden, positions, weights, turned, plan, w_t, b_t, gamma, beta, embed, out_bias)
+
+        def packed_form(sent, *args):
+            return body(True, PACKED_ROWS, sent, *args)
+
+        def whole_form(sent, *args):
+            return body(False, labels.size, None, *args)
+
+        return lax.cond(fits, packed_form, whole_form, sent, *args)
 
     in_specs = (P("dp", None, None), P("dp", None), P("dp", None), P("dp", None), P(None, None), P(None), P(None), P(None), P("tp", None), P("tp"))
     out_specs = (P(), P("dp", None, None), P(None, None), P(None), P(None), P(None), P("tp", None), P("tp"))

time: 469 us -> 420 us (0.90)
  waiting for transfers between devices: 48.7 us -> 8.21 us
  blocking collectives: 38.1 us -> 23.8 us
  starting transfers between devices: 0.46 us -> 6.56 us
    psum x1, waiting for transfers between devices: 34.3 us -> 0.02 us  [body(): d_normed = lax.psum(dt_part, 'tp')]
    all_gather x1 -> x0, blocking collectives: 14.9 us -> none  [local_step(): small = lax.all_gather(small, 'dp', axis=0)]
    ppermute x0 -> x3, starting transfers between devices: none -> 6.19 us  [local_step(): lax.ppermute(small, 'dp', ring)]
    all_gather x1, waiting for transfers between devices: 10.2 us -> 4.15 us  [body(): t_all = lax.all_gather(t_part, ('dp', 'tp'), axis=0, tiled=True)]
    reduce_sum x9 -> x10, other arithmetic: 16.4 us -> 15.5 us  [the longest x1 5.84 us: body(): d_gamma = jnp.sum(d_normed * unit, axis=0)]
  transfers between devices with their start and end apart: 4 -> 7, of which waited for: 3 -> 3; matrix products, arithmetic and copies ran while one was open for 10% -> 18% of each run, Pallas kernels for 53% -> 61%
where the time goes in v4:
time: 420 us; the launch traced here: 413 us
  Pallas kernels  253 us (60%)
  other arithmetic  36.8 us (9%)
  matrix products  33.4 us (8%)
  local copies, waits for them, and re-layouts  29.7 us (7%)
  blocking collectives  23.8 us (6%)
  between operations  16 us (4%)
  waiting for transfers between devices  8.21 us (2%)
  starting transfers between devices  6.56 us (2%)
  loops' own time  5.38 us (1%)
    pallas_call x3, Pallas kernels, de_call(): pl.pallas_call(functools.partial(de_kernel, unrolled, first, part), grid_...  95.6 us
    pallas_call x2, Pallas kernels, logits_call(): pl.pallas_call(functools.partial(logits_kernel, unrolled), grid_spec=pltp...  82.6 us
    pallas_call x2, Pallas kernels, pick(): pl.pallas_call(pick_kernel, grid_spec=pltpu.PrefetchScalarGridSpec(num_sc...  31.5 us
    all_gather x2, blocking collectives, combine(): parts = lax.all_gather(stat[:3], 'tp', axis=0)  23.8 us
    pallas_call x1, Pallas kernels, put(): pl.pallas_call(put_kernel, grid_spec=pltpu.PrefetchScalarGridSpec(num_sca...  21.5 us
    pallas_call x1, Pallas kernels, dt_call(): pl.pallas_call(functools.partial(dt_kernel, unrolled), grid=(slots // blo...  21.4 us
    dot_general x1, matrix products, body(): pre_act = jnp.dot(tok_rows, w_t, preferred_element_type=jnp.float32) + b_t  20.6 us
  transfers between devices with their start and end apart: 7, of which 3 were waited for; matrix products, arithmetic and copies ran while one was open for 18% of the time, Pallas kernels for 61%

profile of v4, /device:TPU:0, one launch (start us, length us, event | category | flops | bytes accessed | tf_op | source)
XLA Modules:
  0.0 412.5 jit_solution(10303344333696207278)
XLA Ops:
  7.2 0.7 convert_element_type.144
  8.1 0.8 copy.119
  9.1 4.2 %collective-permute-start.1 = (f32[2,2560]{1,0:T(2,128)S(1)}, f32[2,2560]{1,0:T(2,128)S(1)}, u32[]{:S(2)}, u32[]{:S(2)}) collective-permute-start(f32[2,2560]{1,0:T(2,128)S(1)} %get-tuple-element.322), channel_id=1, source_target_pairs={{16,0},{24,8},{0,16},{8,24},{17,1},{25,9},{1,17},{9,25},{18,2},{26... | collective-permute-start | bytes 61448 | tf_op jit(solution)/shard_map/ppermute | solution.py:425
  13.2 1.3 collective-permute-start
  14.6 0.7 collective-permute-start.2
  15.3 0.7 reduce_sum.437
  16.5 0.8 copy.121
  17.7 0.6 copy.122.seat_ref
  18.3 1.5 copy.123.rowpos_ref
  19.8 0.6 fusion.61.bounds_ref
  20.4 8.1 %pick.7 = bf16[1536,1024]{1,0:T(8,128)(2,1)} custom-call(s32[2]{0:T(128)} %fusion.61.bounds_ref, s32[128]{0:T(128)S(1)} %convert_element_type.147.off_ref, s32[16,1,160]{2,1,0:T(1,128)} %copy.122.seat_ref, s32[2560,1]{1,0:T(8,128)} %copy.123.rowpos_ref, bf16[16384,1024]{1,0:T(8,128)(2,1)} %bitcast.131), custom_call_target="tpu_custom_call" | custom-call | flops 5905580032 | bytes 33554432 | tf_op jit(solution)/shard_map/pick/pallas_call | solution.py:79
  28.6 4.1 fusion.79
  32.7 0.2 multiply_reduce_fusion.11
  33.0 0.2 fusion.59
  33.4 0.6 reduce_max.45
  34.7 365.1 %conditional.1 = (f32[3824,1024]{1,0:T(8,128)}, f32[]{:T(128)}, bf16[128,128,1024]{2,1,0:T(8,128)(2,1)}, f32[1024,1024]{1,0:T(8,128)}, f32[1024]{0:T(1024)}, /*i...) conditional(s32[]{:T(128)} %convert_element_type.146, (s32[128]{0:T(128)S(1)}, f32[128,20]{0,1:T(8,128)S(1)}, ...), branch_computations={%region_8.36_spmd, %region_36.59_spmd} | conditional | flops 210596691968 | bytes 960796480 | solution.py:443
  38.2 0.8 copy-done.3
  39.0 0.6 copy.128.seat_ref
  39.8 0.3 squeeze.52
  40.8 1.7 select_reduce_fusion.4
  42.5 0.6 reduce_sum.414.lab_ref
  43.1 1.5 copy.129.rowpos_ref
  44.6 1.9 reshape.547.bias_ref
  46.5 23.4 %pick.6 = bf16[1536,1024]{1,0:T(8,128)(2,1)} custom-call(s32[2]{0:T(128)S(1)} %get-tuple-element.103.bounds_ref, s32[128]{0:T(128)S(1)} %get-tuple-element.104.off_ref, s32[16,1,160]{2,1,0:T(1,128)} %copy.128.seat_ref, s32[2560,1]{1,0:T(8,128)} %copy.129.rowpos_ref, bf16[16384,1024]{1,0:T(8,128)(2,1)} %bitcast.134), custom_call_target="tpu_custom_call" | custom-call | flops 5905580032 | bytes 33554432 | tf_op jit(solution)/shard_map/cond/branch_1_fun/pick/pallas_call | solution.py:79
  69.9 20.6 %multiply_add_fusion.1 = (f32[1536,1024]{1,0:T(8,128)}, f32[1536,1024]{1,0:T(8,128)S(1)}, f32[1536,1024]{1,0:T(8,128)}) fusion(f32[1024]{0:T(1024)S(1)} %get-tuple-element.113, bf16[1536,1024]{1,0:T(8,128)(2,1)} %pick.6, bf16[1024,1024]{1,0:T(8,128)(2,1)} %get-tuple-element.112), kind=kOutput, calls=%fused_computation.110 | convolution fusion | flops 3329753088 | bytes 24121344 | tf_op jit(solution)/shard_map/cond/branch_1_fun/dot_general | solution.py:368
  90.4 3.8 fusion.71
  94.3 0.8 multiply_reduce_fusion.8
  95.1 4.3 %add_convert_fusion.3 = (bf16[1536,1024]{1,0:T(8,128)(2,1)}, f32[1536,1024]{1,0:T(8,128)}) fusion(f32[1024]{0:T(1024)S(1)} %get-tuple-element.115, f32[1024]{0:T(1024)S(1)} %get-tuple-element.114, f32[1536]{0:T(1024)S(1)} %add_rsqrt_fusion.2, f32[1536,1024]{1,0:T(8,128)S(1)} %get-tuple-element.278, f32[1536]{0:T(1024)S(1)} %broadcast_multiply_fusion.6), kind=kLoop, calls=%fused_computation.111 | loop fusion | flops 7864320 | bytes 15749120 | tf_op jit(solution)/shard_map/cond/branch_1_fun/convert_element_type | solution.py:374
  99.4 24.3 %logits.6 = (f32[3824,1536]{1,0:T(8,128)}, f32[8,1536]{1,0:T(8,128)}) custom-call(s32[1]{0:T(128)} %bitcast.17.which_ref, bf16[1536,1024]{1,0:T(8,128)(2,1)} %get-tuple-element.275.t_ref, bf16[3824,1024]{1,0:T(8,128)(2,1)} %get-tuple-element.116.embed_ref, f32[3824,1]{1,0:T(8,128)} %reshape.547.bias_ref, s32[1,1536]{1,0:T(1,128)} %reduce_sum.414.lab_ref), custom_call_target="tpu_custom_call" | custom-call | flops 12029263872 | bytes 23494656 | tf_op jit(solution)/shard_map/cond/branch_1_fun/logits/pallas_call | solution.py:170
  123.7 0.8 slice_bitcast_fusion.5
  124.5 10.8 %all-gather.6 = f32[8,3,1536]{2,1,0:T(4,128)S(1)} all-gather(f32[1,3,1536]{2,1,0:T(4,128)S(1)} %slice_bitcast_fusion.5), channel_id=4, replica_groups=mesh['dp'=4,'tp'=8] {'tp'}, dimensions={0}, use_global_device_ids=true | all-gather | bytes 165888 | tf_op jit(solution)/shard_map/cond/branch_1_fun/all_gather | solution.py:315
  135.4 0.6 slice_reduce_fusion.9
  136.9 0.6 multiply_reduce_fusion.10
  137.5 0.7 stack.33.stat_ref
  138.2 21.4 %dt.3 = f32[1536,1024]{1,0:T(8,128)} custom-call(f32[3824,1536]{1,0:T(8,128)} %get-tuple-element.119.z_ref, f32[8,1536]{1,0:T(8,128)} %stack.33.stat_ref, s32[1,1536]{1,0:T(1,128)} %reduce_sum.414.lab_ref, bf16[3824,1024]{1,0:T(8,128)(2,1)} %get-tuple-element.116.embed_ref), custom_call_target="tpu_custom_call" | custom-call | flops 12029263872 | bytes 23494656 | tf_op jit(solution)/shard_map/cond/branch_1_fun/dt/pallas_call | solution.py:214
  159.8 26.1 %de.9 = (f32[3824,1024]{1,0:T(8,128)}, f32[3824,128]{1,0:T(8,128)}) custom-call(s32[1]{0:T(128)} %bitcast.17.which_ref, f32[3824,1536]{1,0:T(8,128)} %get-tuple-element.119.z_ref, f32[8,1536]{1,0:T(8,128)} %stack.33.stat_ref, s32[1,1536]{1,0:T(1,128)} %reduce_sum.414.lab_ref, bf16[1536,1024]{1,0:T(8,128)(2,1)} %get-tuple-element.275.t_ref), custom_call_target="tpu_custom_call" | custom-call | flops 12029263872 | bytes 23494656 | tf_op jit(solution)/shard_map/cond/branch_1_fun/de/pallas_call | solution.py:297
  185.9 0.2 eq.74
  186.1 5.8 %select_reduce_fusion.3 = s32[3,1536]{1,0:T(4,128)S(1)} fusion(s32[3,2560]{1,0:T(4,128)S(1)} %slice_bitcast_fusion.4, s32[3,2560]{1,0:T(4,128)S(1)} %eq.74), kind=kLoop, calls=%fused_computation.101 | loop fusion | flops 35384832 | bytes 79872 | tf_op jit(solution)/shard_map/cond/branch_1_fun/reduce_sum | solution.py:326
  191.9 0.6 copy.144
  192.6 4.2 %all-gather.17.cloned.1.call-done.t_ref = f32[6144,1024]{1,0:T(8,128)} async-done(((f32[192,1024]{1,0:T(8,128)}), f32[6144,1024]{1,0:T(8,128)}) %all-gather.17.cloned.1.call-update) | async-done | bytes 25165840 | tf_op jit(solution)/shard_map/cond/branch_1_fun/all_gather | solution.py:362
  196.7 58.3 %logits.7 = (f32[3824,4608]{1,0:T(8,128)}, f32[8,4608]{1,0:T(8,128)}) custom-call(s32[1]{0:T(128)} %bitcast.17.which_ref, f32[6144,1024]{1,0:T(8,128)} %all-gather.17.cloned.1.call-done.t_ref, bf16[3824,1024]{1,0:T(8,128)(2,1)} %get-tuple-element.116.embed_ref, f32[3824,1]{1,0:T(8,128)} %reshape.547.bias_ref, s32[1,4608]{1,0:T(1,128)} %bitcast.142), custom_call_target="tpu_custom_call" | custom-call | flops 36087791616 | bytes 70483968 | tf_op jit(solution)/shard_map/cond/branch_1_fun/logits/pallas_call | solution.py:170
  255.0 0.9 slice_bitcast_fusion.3
  255.9 13.0 %all-gather.7 = f32[8,3,4608]{2,1,0:T(4,128)S(1)} all-gather(f32[1,3,4608]{2,1,0:T(4,128)S(1)} %slice_bitcast_fusion.3), channel_id=5, replica_groups=mesh['dp'=4,'tp'=8] {'tp'}, dimensions={0}, use_global_device_ids=true | all-gather | bytes 497664 | tf_op jit(solution)/shard_map/cond/branch_1_fun/all_gather | solution.py:315
  269.0 0.3 fusion.76
  269.4 0.8 stack.35.stat_ref
  270.2 34.7 %de.10 = (f32[3824,1024]{1,0:T(8,128)}, f32[3824,128]{1,0:T(8,128)}) custom-call(s32[1]{0:T(128)} %bitcast.17.which_ref, f32[3824,4608]{1,0:T(8,128)} %get-tuple-element.125.z_ref, f32[8,4608]{1,0:T(8,128)} %stack.35.stat_ref, s32[1,4608]{1,0:T(1,128)} %bitcast.143, ...), custom_call_target="tpu_custom_call", output_to_operand_aliasing={{0}: (5, {}), {1}: (6, {})} | custom-call | flops 18043895808 | bytes 35241984 | tf_op jit(solution)/shard_map/cond/branch_1_fun/de/pallas_call | solution.py:297
  305.0 5.8 %multiply_reduce_fusion.6 = (f32[1024]{0:T(1024)S(1)}, f32[1536]{0:T(1024)S(1)}, f32[1536]{0:T(1024)S(1)}, f32[1024]{0:T(1024)S(1)}) fusion(f32[1536,1024]{1,0:T(8,128)} %all-reduce.9.cloned.1.call-done, f32[1536,1024]{1,0:T(8,128)} %get-tuple-element.131, f32[1024]{0:T(1024)S(1)} %get-tuple-element.114), kind=kLoop, calls=%fused_computation.107 | loop fusion | flops 11004928 | bytes 12607488 | tf_op jit(solution)/shard_map/cond/branch_1_fun/reduce_sum | solution.py:403
  310.9 0.6 copy-done.1
  311.4 5.6 %fusion.69 = (f32[1024]{0:T(1024)S(1)}, bf16[1536,1024]{1,0:T(8,128)(2,1)S(1)}) fusion(f32[1536,1024]{1,0:T(8,128)} %get-tuple-element.132, f32[1536]{0:T(1024)S(1)} %add_rsqrt_fusion.2, f32[1536,1024]{1,0:T(8,128)} %get-tuple-element.131, f32[1536]{0:T(1024)S(1)} %get-tuple-element.319, f32[1536]{0:T(1024)S(1)} %get-tuple-element.320, ...), kind=kLoop, calls=%fused_computation.215 | loop fusion | flops 12581888 | bytes 22046720 | tf_op jit(solution)/shard_map/cond/branch_1_fun/reduce_sum | solution.py:409
  317.0 2.4 fusion.38
  319.4 0.6 broadcast_in_dim.138
  320.1 2.4 concatenate.5
  322.5 0.3 all-gather.19.cloned.1.call-start
  322.8 34.7 %de.11 = (f32[3824,1024]{1,0:T(8,128)}, f32[3824,128]{1,0:T(8,128)}) custom-call(s32[1]{0:T(128)} %bitcast.17.which_ref, f32[3824,4608]{1,0:T(8,128)} %get-tuple-element.125.z_ref, f32[8,4608]{1,0:T(8,128)} %stack.35.stat_ref, s32[1,4608]{1,0:T(1,128)} %bitcast.144, ...), custom_call_target="tpu_custom_call", output_to_operand_aliasing={{0}: (5, {}), {1}: (6, {})} | custom-call | flops 18043895808 | bytes 35241984 | tf_op jit(solution)/shard_map/cond/branch_1_fun/de/pallas_call | solution.py:297
  357.5 3.9 all-reduce.11.cloned.1.call-done
  361.4 1.9 slice.151
  363.4 0.7 reshape.545.rowpos_ref
  364.1 1.5 reshape.544.seat_ref
  365.5 1.2 slice.150
  367.4 2.7 reduce_sum.427
  370.1 1.5 fusion.77
  371.6 6.4 %convolution_convert_fusion.1.dh_ref = bf16[1536,1024]{1,0:T(8,128)(2,1)} fusion(bf16[1536,1024]{1,0:T(8,128)(2,1)S(1)} %get-tuple-element.143, bf16[1024,1024]{1,0:T(8,128)(2,1)} %get-tuple-element.112), kind=kOutput, calls=%fused_computation.129 | convolution fusion | flops 3222798336 | bytes 8388608 | tf_op jit(solution)/shard_map/cond/branch_1_fun/ne,de->nd/dot_general | solution.py:415
  378.0 21.5 %put.3 = bf16[16384,1024]{1,0:T(8,128)(2,1)} custom-call(s32[128]{0:T(128)S(1)} %copy-done.26, s32[2560,1]{1,0:T(8,128)} %reshape.544.seat_ref, s32[16,1,160]{2,1,0:T(1,128)} %reshape.545.rowpos_ref, bf16[1536,1024]{1,0:T(8,128)(2,1)} %convolution_convert_fusion.1.dh_ref), custom_call_target="tpu_custom_call" | custom-call | flops 5905580032 | bytes 33554432 | tf_op jit(solution)/shard_map/cond/branch_1_fun/put/pallas_call | solution.py:113
  399.8 4.8 %copy.207 = f32[1024,1024]{1,0:T(8,128)} copy(f32[1024,1024]{1,0:T(8,128)} %get-tuple-element.359) | data formatting | bytes 8388608
  (94 shorter events, 3.0 us)
Async XLA Ops:
  9.1 24.1 %collective-permute-start.1 = (f32[2,2560]{1,0:T(2,128)S(1)}, f32[2,2560]{1,0:T(2,128)S(1)}, u32[]{:S(2)}, u32[]{:S(2)}) collective-permute-start(f32[2,2560]{1,0:T(2,128)S(1)} %get-tuple-element.322), channel_id=1, source_target_pairs={{16,0},{24,8},{0,16},{8,24},{17,1},{25,9},{1,17},{9,25},{18,2},{26... | collective-permute-start | bytes 61448 | tf_op jit(solution)/shard_map/ppermute | solution.py:425
  13.2 20.0 %collective-permute-start = (f32[2,2560]{1,0:T(2,128)S(1)}, f32[2,2560]{1,0:T(2,128)S(1)}, u32[]{:S(2)}, u32[]{:S(2)}) collective-permute-start(f32[2,2560]{1,0:T(2,128)S(1)} %get-tuple-element.322), channel_id=1, source_target_pairs={{8,0},{16,8},{24,16},{0,24},{9,1},{17,9},{25,17},{1,25},{10,2},{18... | collective-permute-start | bytes 61448 | tf_op jit(solution)/shard_map/ppermute | solution.py:425
  14.6 18.6 %collective-permute-start.2 = (f32[2,2560]{1,0:T(2,128)S(1)}, f32[2,2560]{1,0:T(2,128)S(1)}, u32[]{:S(2)}, u32[]{:S(2)}) collective-permute-start(f32[2,2560]{1,0:T(2,128)S(1)} %get-tuple-element.322), channel_id=1, source_target_pairs={{24,0},{0,8},{8,16},{16,24},{25,1},{1,9},{9,17},{17,25},{26,2},{2,... | collective-permute-start | bytes 61448 | tf_op jit(solution)/shard_map/ppermute | solution.py:425
  17.4 11.1 %copy-start.6 = (s32[128,20]{1,0:T(8,128)}, s32[128,20]{1,0:T(8,128)S(1)}, u32[]{:S(2)}) copy-start(s32[128,20]{1,0:T(8,128)S(1)} %get-tuple-element.328) | copy-start | bytes 30724
  17.5 11.1 %copy-start.9 = (s32[128,20]{1,0:T(8,128)}, s32[128,20]{1,0:T(8,128)S(1)}, u32[]{:S(2)}) copy-start(s32[128,20]{1,0:T(8,128)S(1)} %get-tuple-element.327) | copy-start | bytes 30724
  20.4 8.1 %copy-start.27 = (f32[1024]{0:T(1024)S(1)}, f32[1024]{0:T(1024)}, u32[]{:S(2)}) copy-start(f32[1024]{0:T(1024)} %param.19) | copy-start | bytes 12292
  28.6 4.4 %copy-start.12 = (f32[1024]{0:T(1024)S(1)}, f32[1024]{0:T(1024)}, u32[]{:S(2)}) copy-start(f32[1024]{0:T(1024)} %param.20) | copy-start | bytes 12292
  28.6 4.4 %copy-start.22 = (f32[1024]{0:T(1024)S(1)}, f32[1024]{0:T(1024)}, u32[]{:S(2)}) copy-start(f32[1024]{0:T(1024)} %param.21) | copy-start | bytes 12292
  28.6 6.1 %copy-start.20 = (f32[128,20]{0,1:T(8,128)S(1)}, f32[128,20]{0,1:T(8,128)}, u32[]{:S(2)}) copy-start(f32[128,20]{0,1:T(8,128)} %param.17) | copy-start | bytes 30724
  28.6 6.1 %copy-start.21 = (f32[3824]{0:T(1024)S(1)}, f32[3824]{0:T(1024)}, u32[]{:S(2)}) copy-start(f32[3824]{0:T(1024)} %param.23) | copy-start | bytes 45892
  38.1 0.9 copy-start.3
  38.1 31.8 %copy-start.25 = (s32[128]{0:T(128)}, s32[128]{0:T(128)S(1)}, u32[]{:S(2)}) copy-start(s32[128]{0:T(128)S(1)} %get-tuple-element.104.off_ref) | copy-start | bytes 1540 | tf_op jit(solution)/shard_map/cond
  38.1 266.9 %copy-start.15 = (f32[1024]{0:T(1024)}, f32[1024]{0:T(1024)S(1)}, u32[]{:S(2)}) copy-start(f32[1024]{0:T(1024)S(1)} %get-tuple-element.114) | copy-start | bytes 12292 | tf_op jit(solution)/shard_map/cond
  38.1 158.6 %all-gather.17.cloned.1.call-start = ((), (), s32[]{:S(2)}) async-start(), calls=%async_computation.5 | async-start | bytes 25952256 | tf_op jit(solution)/shard_map/cond/branch_1_fun/all_gather | solution.py:362
  39.0 266.0 %all-reduce.9.cloned.1.call-start = ((), (), s32[]{:S(2)}) async-start(), calls=%async_computation.4 | async-start | bytes 12582912 | tf_op jit(solution)/shard_map/cond/branch_1_fun/psum | solution.py:387
  40.6 119.1 %copy-start.4 = (s32[4,128,20]{2,1,0:T(8,128)}, s32[4,128,20]{2,1,0:T(8,128)S(1)}, u32[]{:S(2)}) copy-start(s32[4,128,20]{2,1,0:T(8,128)S(1)} %add_select_fusion.1) | copy-start | bytes 122884 | tf_op jit(solution)/shard_map/cond
  159.6 201.8 %all-reduce.11.cloned.1.call-start = ((), (), s32[]{:S(2)}) async-start(), calls=%async_computation.6 | async-start | bytes 1114112 | tf_op jit(solution)/shard_map/cond/branch_1_fun/psum | solution.py:411
  159.7 26.2 %slice-start.3 = ((s32[4,128,20]{2,1,0:T(8,128)}), s32[3,128,20]{2,1,0:T(8,128)S(1)}, s32[]{:S(2)}) async-start(s32[4,128,20]{2,1,0:T(8,128)} %copy-done.4), calls=%async_computation.11 | async-start | bytes 393216 | tf_op jit(solution)/shard_map/cond/branch_1_fun/slice | solution.py:389
  305.0 6.4 %copy-start.1 = (f32[1536,1024]{1,0:T(8,128)S(1)}, f32[1536,1024]{1,0:T(8,128)}, u32[]{:S(2)}) copy-start(f32[1536,1024]{1,0:T(8,128)} %all-reduce.9.cloned.1.call-done) | copy-start | bytes 18874372 | tf_op jit(solution)/shard_map/cond
  322.5 40.8 %copy-start.8 = (s32[128,20]{1,0:T(8,128)S(1)}, s32[128,20]{1,0:T(8,128)}, u32[]{:S(2)}) copy-start(s32[128,20]{1,0:T(8,128)} %get-tuple-element.142) | copy-start | bytes 30724 | tf_op jit(solution)/shard_map/cond
  322.5 41.6 %copy-start.11 = (s32[128,20]{1,0:T(8,128)S(1)}, s32[128,20]{1,0:T(8,128)}, u32[]{:S(2)}) copy-start(s32[128,20]{1,0:T(8,128)} %get-tuple-element.141) | copy-start | bytes 30724 | tf_op jit(solution)/shard_map/cond
  322.5 77.0 %all-gather.19.cloned.1.call-start = ((), (), s32[]{:S(2)}) async-start(), calls=%async_computation.7 | async-start | bytes 4718592 | tf_op jit(solution)/shard_map/cond/branch_1_fun/all_gather | solution.py:414
  371.6 6.4 %copy-start.26 = (s32[128]{0:T(128)S(1)}, s32[128]{0:T(128)}, u32[]{:S(2)}) copy-start(s32[128]{0:T(128)} %copy-done.25) | copy-start | bytes 1540 | tf_op jit(solution)/shard_map/cond
Sparse Core Ops, SparseCore 0:
  41.8 154.8 all-gather.16
  200.0 104.5 all-reduce.8
  322.6 38.7 all-reduce.10
  363.5 36.0 all-gather.18
